TPU v7x, 512 devices: a whole 4x8x8 slice. The times are simulated.
512 devices in a mesh: gx: 64 (over z_hi, y, core), gy: 8 (over z_lo, x).
Axes of the slice: x: 4, y: 8, z: 8 (z_hi: 4, z_lo: 2; z = z_hi * 2 + z_lo), core: 2. Of those that a mesh axis runs over, the one named last changes fastest.
Arguments:
- field: bfloat16 [1, 512, 512, 128], P(None, 'gx', 'gy'), may hold values from -6 to 6
- conv_weight: bfloat16 [3, 3, 128, 128], replicated, may hold values from -0.1875 to 0.1875
- qkv_weight: bfloat16 [128, 384], replicated, may hold values from -4 to 4
- out_weight: bfloat16 [128, 128], replicated, may hold values from -0.5 to 0.5
Outputs:
- result: bfloat16 [1, 512, 512, 128], P(None, 'gx', 'gy')
All inputs are finite; a program needn't handle non-finite values.
Results may differ from a plain program's by a relative error of at most 0.0064.
Values may be sent and summed in bfloat16 or wider, within the bound.
No kernel may reach another device: no remote copies, remote signals or barrier semaphores. Data moves between devices by JAX's collectives and lax.ppermute only.
A program may use at most 64 MiB of HBM per device.

v0:
```python
import jax
import jax.numpy as jnp
from jax import lax
from jax.sharding import PartitionSpec as P

HEADS = 4
HEAD = 32


def padded_2(cells, sides, width):
    for axis, dim in sides:
        count = lax.axis_size(axis)
        head = lax.slice_in_dim(cells, 0, width, axis=dim)
        tail = lax.slice_in_dim(cells, cells.shape[dim] - width, cells.shape[dim], axis=dim)
        cells = jnp.concatenate(
            [
                lax.ppermute(tail, axis, [(i, (i + 1) % count) for i in range(count)]),
                cells,
                lax.ppermute(head, axis, [((i + 1) % count, i) for i in range(count)]),
            ],
            axis=dim,
        )
    return cells


def head_attend(parts):
    query, keyed, valued = parts
    scores = jnp.einsum("zqyd,zkyd->zyqk", query, keyed, preferred_element_type=jnp.float32)
    scores = scores / jnp.sqrt(jnp.float32(HEAD))
    top = jnp.max(scores, axis=-1, keepdims=True)
    expo = jnp.exp(scores - top)
    probs = (expo / jnp.sum(expo, axis=-1, keepdims=True)).astype(jnp.bfloat16)
    mixed = jnp.einsum("zyqk,zkyd->zqyd", probs, valued, preferred_element_type=jnp.float32)
    return mixed.astype(jnp.bfloat16)


def split_heads(block):
    planes, length, cols, width = block.shape
    return jnp.moveaxis(block.reshape(planes, length, cols, HEADS, width // HEADS), 3, 0)


def attend_lines(normed, qkv_weight):
    planes, length, cols, width = normed.shape
    qkv = jnp.dot(normed.reshape(-1, width), qkv_weight, preferred_element_type=jnp.float32)
    qkv = qkv.astype(jnp.bfloat16).reshape(planes, length, cols, 3 * width)
    query = split_heads(qkv[..., :width])
    keyed = split_heads(qkv[..., width : 2 * width])
    valued = split_heads(qkv[..., 2 * width :])
    mixed = lax.map(head_attend, (query, keyed, valued))
    return jnp.moveaxis(mixed, 0, 3).reshape(planes, length, cols, width)


def return_cells(block):
    return lax.all_to_all(block, "gx", split_axis=1, concat_axis=2, tiled=True)


def convolve(padded, conv_weight, rows, cols):
    planes = padded.shape[0]
    width = padded.shape[3]
    stem = jnp.zeros((planes, rows, cols, width), jnp.float32)
    for a in range(3):
        for b in range(3):
            window = padded[:, a : a + rows, b : b + cols, :]
            part = jnp.dot(
                window.reshape(-1, width), conv_weight[a, b], preferred_element_type=jnp.float32
            )
            stem = stem + part.reshape(planes, rows, cols, width)
    return stem


def normalize(stem):
    mean = jnp.mean(stem, axis=-1, keepdims=True)
    varia = jnp.mean((stem - mean) ** 2, axis=-1, keepdims=True)
    return ((stem - mean) / jnp.sqrt(varia + 1e-05)).astype(jnp.bfloat16)


def finish(stem, attended, out_weight):
    width = stem.shape[3]
    projected = jnp.dot(attended.reshape(-1, width), out_weight, preferred_element_type=jnp.float32)
    return (stem + projected.reshape(stem.shape)).astype(jnp.bfloat16)


def on_device(field, conv_weight, qkv_weight, out_weight):
    planes, rows, cols, width = field.shape
    padded = padded_2(field, (("gx", 1), ("gy", 2)), 1)
    stem = convolve(padded, conv_weight, rows, cols)
    normed = normalize(stem)
    attended = return_cells(
        attend_lines(
            lax.all_to_all(normed, "gx", split_axis=2, concat_axis=1, tiled=True), qkv_weight
        )
    )
    return finish(stem, attended, out_weight)


def solution(mesh):
    placed = (P(None, "gx", "gy", None), P(), P(), P())
    return jax.shard_map(
        on_device, mesh=mesh, in_specs=placed, out_specs=P(None, "gx", "gy", None), check_vma=False
    )
```

profile of v0, /device:TPU:1, one launch (start us, length us, event | category | flops | bytes accessed | tf_op | source)
XLA Modules:
  0.0 75.9 jit_solution(8873037923194557447)
XLA Ops:
  0.0 0.8 %fusion.78 = (bf16[1,1,64,128]{3,2,1,0:T(8,128)(2,1)S(1)}, bf16[1,1,64,128]{3,2,1,0:T(8,128)(2,1)S(1)}) fusion(bf16[1,8,64,128]{3,2,1,0:T(8,128)(2,1)} %param.6), kind=kLoop, calls=%fused_computation.102 | loop fusion | bytes 65536 | tf_op jit(solution)/shard_map/slice | solution.py:13
  0.8 4.6 %collective-permute-start = (bf16[1,1,64,128]{3,2,1,0:T(8,128)(2,1)S(1)}, bf16[1,1,64,128]{3,2,1,0:T(8,128)(2,1)S(1)}, u32[]{:S(2)}, u32[]{:S(2)}) collective-permute-start(bf16[1,1,64,128]{3,2,1,0:T(8,128)(2,1)S(1)} %get-tuple-element.51), channel_id=1, source_target_pairs={{0,8},{8,16},{16,24},{24,32},{32,40},{40,48},{48,56},{56,64},{64,7... | collective-permute-start | bytes 49160 | tf_op jit(solution)/shard_map/ppermute | solution.py:17
  5.4 6.1 %collective-permute-start.1 = (bf16[1,1,64,128]{3,2,1,0:T(8,128)(2,1)S(1)}, bf16[1,1,64,128]{3,2,1,0:T(8,128)(2,1)S(1)}, u32[]{:S(2)}, u32[]{:S(2)}) collective-permute-start(bf16[1,1,64,128]{3,2,1,0:T(8,128)(2,1)S(1)} %get-tuple-element.50), channel_id=1, source_target_pairs={{8,0},{16,8},{24,16},{32,24},{40,32},{48,40},{56,48},{64,56},{72,6... | collective-permute-start | bytes 49160 | tf_op jit(solution)/shard_map/ppermute | solution.py:19
  11.5 0.0 collective-permute-done
  11.5 0.0 copy-start.1
  11.5 1.0 %constant_dynamic-update-slice_fusion.1 = bf16[1,10,64,128]{3,2,1,0:T(8,128)(2,1)S(1)} fusion(bf16[1,10,64,128]{3,2,1,0:T(8,128)(2,1)S(1)} %constant_dynamic-update-slice_fusion.2, bf16[1,8,64,128]{3,2,1,0:T(8,128)(2,1)} %param.6), kind=kLoop, calls=%fused_computation.87 | loop fusion | bytes 262144
  12.5 0.0 copy-start.2
  12.6 2.1 %collective-permute-start.2 = (bf16[1,10,1,128]{3,2,1,0:T(2,128)(2,1)S(1)}, bf16[1,10,1,128]{3,2,1,0:T(2,128)(2,1)S(1)}, u32[]{:S(2)}, u32[]{:S(2)}) collective-permute-start(bf16[1,10,1,128]{3,2,1,0:T(2,128)(2,1)S(1)} %get-tuple-element.48), channel_id=1, source_target_pairs={{0,1},{1,2},{2,3},{3,4},{4,5},{5,6},{6,7},{7,0},{8,9},{9,10},{10,1... | collective-permute-start | bytes 7688 | tf_op jit(solution)/shard_map/ppermute | solution.py:17
  14.6 5.5 %collective-permute-start.3 = (bf16[1,10,1,128]{3,2,1,0:T(2,128)(2,1)S(1)}, bf16[1,10,1,128]{3,2,1,0:T(2,128)(2,1)S(1)}, u32[]{:S(2)}, u32[]{:S(2)}) collective-permute-start(bf16[1,10,1,128]{3,2,1,0:T(2,128)(2,1)S(1)} %get-tuple-element.49), channel_id=1, source_target_pairs={{1,0},{2,1},{3,2},{4,3},{5,4},{6,5},{7,6},{0,7},{9,8},{10,9},{11,1... | collective-permute-start | bytes 7688 | tf_op jit(solution)/shard_map/ppermute | solution.py:19
  20.1 0.9 %fusion.40 = f32[8,64,128]{2,1,0:T(8,128)S(1)} fusion(bf16[1,8,64,128]{3,2,1,0:T(8,128)(2,1)S(1)} %copy-done.1, bf16[1,1,64,128]{3,2,1,0:T(8,128)(2,1)S(1)} %collective-permute-done, bf16[3,3,128,128]{3,2,1,0:T(8,128)(2,1)} %param.7), kind=kOutput, calls=%fused_computation.59 | convolution fusion | flops 16842752 | bytes 442368 | tf_op jit(solution)/shard_map/dot_general | solution.py:64
  21.1 0.2 fusion.33
  21.2 0.0 collective-permute-done.2
  21.2 0.2 convolution_add_fusion.6
  21.4 0.0 collective-permute-done.3
  21.4 0.2 convolution_add_fusion.5
  21.6 0.2 convolution_add_fusion.4
  21.8 0.2 convolution_add_fusion.3
  22.0 0.2 fusion.29
  22.1 0.2 convolution_add_fusion.2
  22.3 0.3 fusion.79
  22.6 0.3 multiply_reduce_fusion
  22.9 0.2 fusion.47
  23.1 0.7 copy.21
  23.9 14.6 %all-to-all-start = ((bf16[1,8,64,128]{3,1,0,2:T(8,128)(2,1)}), bf16[1,8,64,128]{3,1,0,2:T(8,128)(2,1)S(1)}, u32[]{:S(2)}, u32[]{:S(2)}) async-start(bf16[1,8,64,128]{3,1,0,2:T(8,128)(2,1)} %copy.21), calls=%async_computation | async-start | bytes 262144 | tf_op jit(solution)/shard_map/all_to_all | solution.py:90
  38.5 12.8 %all-to-all-done = bf16[1,8,64,128]{3,1,0,2:T(8,128)(2,1)S(1)} async-done(((bf16[1,8,64,128]{3,1,0,2:T(8,128)(2,1)}), bf16[1,8,64,128]{3,1,0,2:T(8,128)(2,1)S(1)}, u32[]{:S(2)}, u32[]{:S(2)}) %all-to-all-start) | async-done | bytes 131104 | tf_op jit(solution)/shard_map/all_to_all | solution.py:90
  51.3 0.3 fusion.11
  51.6 3.4 %while.10 = (s32[]{:T(128)}, bf16[4,1,512,1,32]{2,4,3,1,0:T(8,128)(2,1)S(1)}, bf16[4,1,512,1,32]{2,4,3,1,0:T(8,128)(2,1)S(1)}, bf16[4,1,512,1,32]{2,4,3,1,0:T(8,...) while((s32[]{:T(128)}, bf16[4,1,512,1,32]{2,4,3,1,0:T(8,128)(2,1)S(1)}, ...), condition=%wide.region_5.6_spmd, body=%wide.region_2.5_spmd.sunk | while | flops 35404800 | bytes 3289157 | solution.py:49
  51.6 0.4 fusion.86
  52.0 0.2 fusion.87
  52.2 0.3 fusion.88
  52.5 0.4 fusion.86
  52.8 0.2 fusion.87
  53.0 0.3 fusion.88
  53.3 0.4 fusion.86
  53.7 0.2 fusion.87
  53.9 0.3 fusion.88
  54.2 0.4 fusion.86
  54.6 0.2 fusion.87
  54.8 0.3 fusion.88
  55.0 0.2 copy.26
  55.2 0.5 broadcast.39
  55.7 1.4 %reduce.8 = bf16[512,128]{1,0:T(8,128)(2,1)S(1)} reduce(bf16[512,1,1,128]{3,2,1,0:T(2,128)(2,1)S(1)} %bitcast.152, bf16[]{:T(256)} %broadcast.39), dimensions={1,2}, to_apply=%bitcast.132.reduce_sub_computation | reduce | bytes 262146
  57.2 0.1 reshape.154
  57.2 17.0 %all_to_all.30 = bf16[64,2,512]{2,1,0:T(2,128)(2,1)S(1)} all-to-all(bf16[64,2,512]{2,1,0:T(2,128)(2,1)S(1)} %reshape.154), channel_id=1, replica_groups=mesh['gx'=64,'gy'=8] {'gx'}, dimensions={0} | all-to-all | bytes 262144 | tf_op jit(solution)/shard_map/all_to_all | solution.py:54
  74.2 0.1 reshape.155
  74.3 0.0 copy-start.3
  74.4 0.7 copy-done.3
  75.1 0.8 %fusion.15 = bf16[1,8,64,128]{3,2,1,0:T(8,128)(2,1)} fusion(f32[8,64,128]{2,1,0:T(8,128)S(1)} %get-tuple-element.53, bf16[1,64,8,1,128]{4,2,1,3,0:T(8,128)(2,1)S(1)} %bitcast.156, bf16[128,128]{1,0:T(8,128)(2,1)S(1)} %copy-done.3), kind=kOutput, calls=%fused_computation.27 | convolution fusion | flops 16908288 | bytes 557056 | tf_op jit(solution)/shard_map/dot_general | solution.py:79
  (13 shorter events, 0.1 us)
Async XLA Ops:
  0.0 51.3 %copy-start = (bf16[128,384]{1,0:T(8,128)(2,1)S(1)}, bf16[128,384]{1,0:T(8,128)(2,1)}, u32[]{:S(2)}) copy-start(bf16[128,384]{1,0:T(8,128)(2,1)} %param.8) | copy-start | bytes 294916
  0.8 10.7 %collective-permute-start = (bf16[1,1,64,128]{3,2,1,0:T(8,128)(2,1)S(1)}, bf16[1,1,64,128]{3,2,1,0:T(8,128)(2,1)S(1)}, u32[]{:S(2)}, u32[]{:S(2)}) collective-permute-start(bf16[1,1,64,128]{3,2,1,0:T(8,128)(2,1)S(1)} %get-tuple-element.51), channel_id=1, source_target_pairs={{0,8},{8,16},{16,24},{24,32},{32,40},{40,48},{48,56},{56,64},{64,7... | collective-permute-start | bytes 49160 | tf_op jit(solution)/shard_map/ppermute | solution.py:17
  5.4 7.2 %collective-permute-start.1 = (bf16[1,1,64,128]{3,2,1,0:T(8,128)(2,1)S(1)}, bf16[1,1,64,128]{3,2,1,0:T(8,128)(2,1)S(1)}, u32[]{:S(2)}, u32[]{:S(2)}) collective-permute-start(bf16[1,1,64,128]{3,2,1,0:T(8,128)(2,1)S(1)} %get-tuple-element.50), channel_id=1, source_target_pairs={{8,0},{16,8},{24,16},{32,24},{40,32},{48,40},{56,48},{64,56},{72,6... | collective-permute-start | bytes 49160 | tf_op jit(solution)/shard_map/ppermute | solution.py:19
  11.5 8.6 %copy-start.1 = (bf16[1,8,64,128]{3,2,1,0:T(8,128)(2,1)S(1)}, bf16[1,8,64,128]{3,2,1,0:T(8,128)(2,1)}, u32[]{:S(2)}) copy-start(bf16[1,8,64,128]{3,2,1,0:T(8,128)(2,1)} %param.6) | copy-start | bytes 393220
  12.5 8.5 %copy-start.2 = (bf16[3,3,128,128]{3,2,1,0:T(8,128)(2,1)S(1)}, bf16[3,3,128,128]{3,2,1,0:T(8,128)(2,1)}, u32[]{:S(2)}) copy-start(bf16[3,3,128,128]{3,2,1,0:T(8,128)(2,1)} %param.7) | copy-start | bytes 884740
  12.6 8.7 %collective-permute-start.2 = (bf16[1,10,1,128]{3,2,1,0:T(2,128)(2,1)S(1)}, bf16[1,10,1,128]{3,2,1,0:T(2,128)(2,1)S(1)}, u32[]{:S(2)}, u32[]{:S(2)}) collective-permute-start(bf16[1,10,1,128]{3,2,1,0:T(2,128)(2,1)S(1)} %get-tuple-element.48), channel_id=1, source_target_pairs={{0,1},{1,2},{2,3},{3,4},{4,5},{5,6},{6,7},{7,0},{8,9},{9,10},{10,1... | collective-permute-start | bytes 7688 | tf_op jit(solution)/shard_map/ppermute | solution.py:17
  14.6 6.8 %collective-permute-start.3 = (bf16[1,10,1,128]{3,2,1,0:T(2,128)(2,1)S(1)}, bf16[1,10,1,128]{3,2,1,0:T(2,128)(2,1)S(1)}, u32[]{:S(2)}, u32[]{:S(2)}) collective-permute-start(bf16[1,10,1,128]{3,2,1,0:T(2,128)(2,1)S(1)} %get-tuple-element.49), channel_id=1, source_target_pairs={{1,0},{2,1},{3,2},{4,3},{5,4},{6,5},{7,6},{0,7},{9,8},{10,9},{11,1... | collective-permute-start | bytes 7688 | tf_op jit(solution)/shard_map/ppermute | solution.py:19
  23.9 27.4 %all-to-all-start = ((bf16[1,8,64,128]{3,1,0,2:T(8,128)(2,1)}), bf16[1,8,64,128]{3,1,0,2:T(8,128)(2,1)S(1)}, u32[]{:S(2)}, u32[]{:S(2)}) async-start(bf16[1,8,64,128]{3,1,0,2:T(8,128)(2,1)} %copy.21), calls=%async_computation | async-start | bytes 262144 | tf_op jit(solution)/shard_map/all_to_all | solution.py:90
  74.3 0.8 %copy-start.3 = (bf16[128,128]{1,0:T(8,128)(2,1)S(1)}, bf16[128,128]{1,0:T(8,128)(2,1)}, u32[]{:S(2)}) copy-start(bf16[128,128]{1,0:T(8,128)(2,1)} %param.9) | copy-start | bytes 98308
where the time goes:
time: 76.9 us; the launch traced here: 75.9 us
  starting transfers between devices  32.8 us (43%)
  blocking collectives  17 us (22%)
  waiting for transfers between devices  12.8 us (17%)
  matrix products  6.14 us (8%)
  local copies, waits for them, and re-layouts  4.16 us (5%)
  other arithmetic  2.67 us (3%)
    all_to_all x1, blocking collectives, return_cells(): return lax.all_to_all(block, 'gx', split_axis=1, concat_axis=2, tiled=True)  17 us
    all_to_all x1, starting transfers between devices, on_device(): lax.all_to_all(normed, 'gx', split_axis=2, concat_axis=1, tiled=True)  14.6 us
    all_to_all x1, waiting for transfers between devices, on_device(): lax.all_to_all(normed, 'gx', split_axis=2, concat_axis=1, tiled=True)  12.8 us
    ppermute x2, starting transfers between devices, padded_2(): lax.ppermute(head, axis, [((i + 1) % count, i) for i in range(count)])  11.6 us
    ppermute x2, starting transfers between devices, padded_2(): lax.ppermute(tail, axis, [(i, (i + 1) % count) for i in range(count)])  6.63 us
    unnamed x14, local copies, waits for them, and re-layouts  2.42 us
    dot_general x9, matrix products, convolve(): jnp.dot(window.reshape(-1, width), conv_weight[a, b], preferred_element_t...  2.41 us
  transfers between devices with their start and end apart: 5, of which 1 were waited for; matrix products, arithmetic and copies ran while one was open for 3% of the time, Pallas kernels for 0%

commit v1 on v0

v1 whole, which is shorter than its diff:
```python
import jax
import jax.numpy as jnp
from jax import lax
from jax.sharding import PartitionSpec as P

HEADS = 4
HEAD = 32


def to_lines(block):
    return lax.all_to_all(block, "gx", split_axis=2, concat_axis=1, tiled=True)


def to_blocks(lines):
    return lax.all_to_all(lines, "gx", split_axis=1, concat_axis=2, tiled=True)


def neighbour_lines(line):
    n_gx, n_gy = lax.axis_size("gx"), lax.axis_size("gy")
    count = n_gx * n_gy

    def device(c):
        c = c % count
        return (c % n_gx) * n_gy + c // n_gx

    from_left = lax.ppermute(line, ("gx", "gy"), [(device(c), device(c + 1)) for c in range(count)])
    from_right = lax.ppermute(line, ("gx", "gy"), [(device(c + 1), device(c)) for c in range(count)])
    return from_left, from_right


def convolve(columns, conv_weight):
    length, width = columns.shape[1], columns.shape[2]
    taps = []
    for a in range(3):
        for b in range(3):
            taps.append(jnp.roll(columns[b], 1 - a, axis=0))
    stacked = jnp.concatenate(taps, axis=1)
    return jnp.dot(
        stacked, conv_weight.reshape(9 * width, width), preferred_element_type=jnp.float32
    )


def normalize(stem):
    mean = jnp.mean(stem, axis=-1, keepdims=True)
    varia = jnp.mean((stem - mean) ** 2, axis=-1, keepdims=True)
    return ((stem - mean) / jnp.sqrt(varia + 1e-05)).astype(jnp.bfloat16)


def attend(normed, qkv_weight):
    length, width = normed.shape
    qkv = jnp.dot(normed, qkv_weight, preferred_element_type=jnp.float32).astype(jnp.bfloat16)
    query = qkv[:, :width].reshape(length, HEADS, HEAD)
    keyed = qkv[:, width : 2 * width].reshape(length, HEADS, HEAD)
    valued = qkv[:, 2 * width :].reshape(length, HEADS, HEAD)
    scores = jnp.einsum("qhd,khd->hqk", query, keyed, preferred_element_type=jnp.float32)
    scores = scores / jnp.sqrt(jnp.float32(HEAD))
    top = jnp.max(scores, axis=-1, keepdims=True)
    expo = jnp.exp(scores - top)
    probs = (expo / jnp.sum(expo, axis=-1, keepdims=True)).astype(jnp.bfloat16)
    mixed = jnp.einsum("hqk,khd->qhd", probs, valued, preferred_element_type=jnp.float32)
    return mixed.astype(jnp.bfloat16).reshape(length, width)


def on_device(field, conv_weight, qkv_weight, out_weight):
    lines = to_lines(field)
    planes, length, _, width = lines.shape
    line = lines.reshape(length, width)
    from_left, from_right = neighbour_lines(line)
    stem = convolve(jnp.stack([from_left, line, from_right]), conv_weight)
    normed = normalize(stem)
    attended = attend(normed, qkv_weight)
    projected = jnp.dot(attended, out_weight, preferred_element_type=jnp.float32)
    result = (stem + projected).astype(jnp.bfloat16)
    return to_blocks(result.reshape(planes, length, 1, width))


def solution(mesh):
    placed = (P(None, "gx", "gy", None), P(), P(), P())
    return jax.shard_map(
        on_device, mesh=mesh, in_specs=placed, out_specs=P(None, "gx", "gy", None), check_vma=False
    )
```

time: 76.9 us -> 78.6 us (1.022)
  blocking collectives: 17 us -> 55.9 us
  starting transfers between devices: 32.8 us -> 5.12 us
  waiting for transfers between devices: 12.8 us -> 4.45 us
  local copies, waits for them, and re-layouts: 4.16 us -> 3.09 us
  matrix products: 6.14 us -> 7.15 us
  other arithmetic: 2.67 us -> 1.74 us
    all_to_all x1 -> x2, blocking collectives: 17 us -> 55.9 us  [the longest x1 30.2 us: to_lines(): return lax.all_to_all(block, 'gx', split_axis=2, concat_axis=1, tiled=True)]
    all_to_all x1 -> x0, starting transfers between devices: 14.6 us -> none  [on_device(): lax.all_to_all(normed, 'gx', split_axis=2, concat_axis=1, tiled=True)]
    ppermute x4 -> x2, starting transfers between devices: 18.2 us -> 5.12 us  [the longest x1 3.2 us: neighbour_lines(): lax.ppermute(line, ('gx', 'gy'), [(device(c), device(c + 1)) for c in ran...]
    all_to_all x1 -> x0, waiting for transfers between devices: 12.8 us -> none  [on_device(): lax.all_to_all(normed, 'gx', split_axis=2, concat_axis=1, tiled=True)]
    ppermute x4 -> x2, waiting for transfers between devices: 0.01 us -> 4.45 us  [the longest x1 4.45 us: neighbour_lines(): lax.ppermute(line, ('gx', 'gy'), [(device(c + 1), device(c)) for c in ran...]
    sub x0 -> x1, matrix products: none -> 3.43 us  [attend(): expo = jnp.exp(scores - top)]
    dot_general x19 -> x4, matrix products: 6.14 us -> 3.72 us  [the longest x1 2.66 us: attend(): jnp.einsum('hqk,khd->qhd', probs, valued, preferred_element_type=jnp.floa...]
    unnamed x1 -> x6, other arithmetic: 1.41 us -> 1.64 us
  transfers between devices with their start and end apart: 5 -> 2, of which waited for: 1 -> 1; matrix products, arithmetic and copies ran while one was open for 3% -> 0% of each run, Pallas kernels for 0% -> 0%
where the time goes in v1:
time: 78.6 us; the launch traced here: 77.7 us
  blocking collectives  55.9 us (71%)
  matrix products  7.15 us (9%)
  starting transfers between devices  5.12 us (7%)
  waiting for transfers between devices  4.45 us (6%)
  local copies, waits for them, and re-layouts  3.09 us (4%)
  other arithmetic  1.74 us (2%)
    all_to_all x1, blocking collectives, to_lines(): return lax.all_to_all(block, 'gx', split_axis=2, concat_axis=1, tiled=True)  30.2 us
    all_to_all x1, blocking collectives, to_blocks(): return lax.all_to_all(lines, 'gx', split_axis=1, concat_axis=2, tiled=True)  25.7 us
    ppermute x1, waiting for transfers between devices, neighbour_lines(): lax.ppermute(line, ('gx', 'gy'), [(device(c + 1), device(c)) for c in ran...  4.45 us
    sub x1, matrix products, attend(): expo = jnp.exp(scores - top)  3.43 us
    ppermute x1, starting transfers between devices, neighbour_lines(): lax.ppermute(line, ('gx', 'gy'), [(device(c), device(c + 1)) for c in ran...  3.2 us
    dot_general x1, matrix products, attend(): jnp.einsum('hqk,khd->qhd', probs, valued, preferred_element_type=jnp.floa...  2.66 us
    unnamed x14, local copies, waits for them, and re-layouts  2.06 us
    ppermute x1, starting transfers between devices, neighbour_lines(): lax.ppermute(line, ('gx', 'gy'), [(device(c + 1), device(c)) for c in ran...  1.92 us
  transfers between devices with their start and end apart: 2, of which 1 were waited for; matrix products, arithmetic and copies ran while one was open for 0% of the time, Pallas kernels for 0%

profile of v1, /device:TPU:1, one launch (start us, length us, event | category | flops | bytes accessed | tf_op | source)
XLA Modules:
  0.0 77.7 jit_solution(10470661683168732793)
XLA Ops:
  0.0 0.0 copy-start
  0.0 1.0 %copy.13 = bf16[1,8,64,128]{3,1,0,2:T(8,128)(2,1)S(1)} copy(bf16[1,8,64,128]{3,2,1,0:T(8,128)(2,1)} %param.4) | data formatting | bytes 262144 | tf_op args[0]
  1.0 30.2 %all_to_all.33 = bf16[1,8,64,128]{3,1,0,2:T(8,128)(2,1)S(1)} all-to-all(bf16[1,8,64,128]{3,1,0,2:T(8,128)(2,1)S(1)} %copy.13), channel_id=1, replica_groups=mesh['gx'=64,'gy'=8] {'gx'}, dimensions={2} | all-to-all | bytes 262144 | tf_op jit(solution)/shard_map/all_to_all | solution.py:11
  31.2 3.2 %collective-permute-start = (bf16[512,128]{1,0:T(8,128)(2,1)S(1)}, bf16[512,128]{1,0:T(8,128)(2,1)S(1)}, u32[]{:S(2)}, u32[]{:S(2)}) collective-permute-start(bf16[512,128]{1,0:T(8,128)(2,1)S(1)} %bitcast.35), channel_id=1, source_target_pairs={{0,8},{8,16},{16,24},{24,32},{32,40},{40,48},{48,56},{56,64},{64,7... | collective-permute-start | bytes 393224 | tf_op jit(solution)/shard_map/ppermute | solution.py:26
  34.5 1.9 %collective-permute-start.1 = (bf16[512,128]{1,0:T(8,128)(2,1)S(1)}, bf16[512,128]{1,0:T(8,128)(2,1)S(1)}, u32[]{:S(2)}, u32[]{:S(2)}) collective-permute-start(bf16[512,128]{1,0:T(8,128)(2,1)S(1)} %bitcast.37), channel_id=1, source_target_pairs={{8,0},{16,8},{24,16},{32,24},{40,32},{48,40},{56,48},{64,56},{72,6... | collective-permute-start | bytes 393224 | tf_op jit(solution)/shard_map/ppermute | solution.py:27
  36.4 0.0 collective-permute-done
  36.6 0.1 maximum_dynamic-update-slice_fusion.4
  36.6 4.4 %collective-permute-done.1 = bf16[512,128]{1,0:T(8,128)(2,1)S(1)} collective-permute-done((bf16[512,128]{1,0:T(8,128)(2,1)S(1)}, bf16[512,128]{1,0:T(8,128)(2,1)S(1)}, u32[]{:S(2)}, u32[]{:S(2)}) %collective-permute-start.1) | collective-permute-done | bytes 131104 | tf_op jit(solution)/shard_map/ppermute | solution.py:27
  41.1 0.1 maximum_dynamic-update-slice_fusion.3
  41.4 0.0 copy-start.2
  41.5 0.0 copy-done
  41.5 0.5 fusion.21
  42.0 0.1 multiply_reduce_fusion.1
  42.1 0.2 copy-done.2
  42.3 0.3 convolution_convert_fusion
  42.7 3.4 %fusion.22 = (f32[4,512]{1,0:T(4,128)S(1)}, f32[4,512,512]{1,2,0:T(8,128)}) fusion(bf16[512,4,32]{0,2,1:T(8,128)(2,1)S(1)} %bitcast.45, bf16[512,4,32]{0,2,1:T(8,128)(2,1)S(1)} %bitcast.44), kind=kOutput, calls=%fused_computation.38 | convolution fusion | flops 70255104 | bytes 4464640 | tf_op jit(solution)/shard_map/sub | solution.py:58
  46.1 0.0 copy-start.1
  46.1 2.7 %fusion.7 = bf16[4,32,512]{2,1,0:T(8,128)(2,1)S(1)} fusion(bf16[512,4,32]{0,2,1:T(8,128)(2,1)S(1)} %bitcast.43, f32[4,512,512]{1,2,0:T(8,128)} %get-tuple-element.23, f32[4,512]{1,0:T(4,128)S(1)} %get-tuple-element.22), kind=kOutput, calls=%fused_computation.10 | convolution fusion | flops 69271552 | bytes 4464640 | tf_op jit(solution)/shard_map/hqk,khd->qhd/dot_general | solution.py:60
  48.7 0.0 copy-done.1
  48.8 0.2 fusion.8
  49.0 0.2 copy.16
  49.2 0.5 broadcast.26
  49.7 1.4 %reduce = bf16[512,128]{1,0:T(8,128)(2,1)S(1)} reduce(bf16[512,1,1,128]{3,2,1,0:T(2,128)(2,1)S(1)} %bitcast.39, bf16[]{:T(256)} %broadcast.26), dimensions={1,2}, to_apply=%bitcast.21.reduce_sub_computation | reduce | bytes 262146
  51.1 0.1 reshape.43
  51.2 25.7 %all_to_all.34 = bf16[64,2,512]{2,1,0:T(2,128)(2,1)S(1)} all-to-all(bf16[64,2,512]{2,1,0:T(2,128)(2,1)S(1)} %reshape.43), channel_id=1, replica_groups=mesh['gx'=64,'gy'=8] {'gx'}, dimensions={0} | all-to-all | bytes 262144 | tf_op jit(solution)/shard_map/all_to_all | solution.py:15
  76.9 0.1 reshape.44
  77.0 0.7 copy.17
  (17 shorter events, 0.5 us)
Async XLA Ops:
  0.0 41.5 %copy-start = (bf16[3,3,128,128]{3,2,1,0:T(8,128)(2,1)S(1)}, bf16[3,3,128,128]{3,2,1,0:T(8,128)(2,1)}, u32[]{:S(2)}) copy-start(bf16[3,3,128,128]{3,2,1,0:T(8,128)(2,1)} %param.5) | copy-start | bytes 884740
  31.2 5.2 %collective-permute-start = (bf16[512,128]{1,0:T(8,128)(2,1)S(1)}, bf16[512,128]{1,0:T(8,128)(2,1)S(1)}, u32[]{:S(2)}, u32[]{:S(2)}) collective-permute-start(bf16[512,128]{1,0:T(8,128)(2,1)S(1)} %bitcast.35), channel_id=1, source_target_pairs={{0,8},{8,16},{16,24},{24,32},{32,40},{40,48},{48,56},{56,64},{64,7... | collective-permute-start | bytes 393224 | tf_op jit(solution)/shard_map/ppermute | solution.py:26
  34.5 6.6 %collective-permute-start.1 = (bf16[512,128]{1,0:T(8,128)(2,1)S(1)}, bf16[512,128]{1,0:T(8,128)(2,1)S(1)}, u32[]{:S(2)}, u32[]{:S(2)}) collective-permute-start(bf16[512,128]{1,0:T(8,128)(2,1)S(1)} %bitcast.37), channel_id=1, source_target_pairs={{8,0},{16,8},{24,16},{32,24},{40,32},{48,40},{56,48},{64,56},{72,6... | collective-permute-start | bytes 393224 | tf_op jit(solution)/shard_map/ppermute | solution.py:27
  41.4 0.9 %copy-start.2 = (bf16[128,384]{1,0:T(8,128)(2,1)S(1)}, bf16[128,384]{1,0:T(8,128)(2,1)}, u32[]{:S(2)}) copy-start(bf16[128,384]{1,0:T(8,128)(2,1)} %param.6) | copy-start | bytes 294916
  46.1 2.7 %copy-start.1 = (bf16[128,128]{1,0:T(8,128)(2,1)S(1)}, bf16[128,128]{1,0:T(8,128)(2,1)}, u32[]{:S(2)}) copy-start(bf16[128,128]{1,0:T(8,128)(2,1)} %param.7) | copy-start | bytes 98308

commit v2 on v1

--- a/solution.py
+++ b/solution.py
@@ -7,25 +7,21 @@
 HEAD = 32
 
 
-def to_lines(block):
-    return lax.all_to_all(block, "gx", split_axis=2, concat_axis=1, tiled=True)
+def padded_columns(block):
+    count = lax.axis_size("gy")
+    left = lax.ppermute(block[:, :, -1:], "gy", [(i, (i + 1) % count) for i in range(count)])
+    right = lax.ppermute(block[:, :, :1], "gy", [((i + 1) % count, i) for i in range(count)])
+    return jnp.concatenate([left, block, right], axis=2)
+
+
+def to_lines(padded):
+    cols = padded.shape[2] - 2
+    windows = jnp.stack([padded[:, :, b : b + cols] for b in range(3)], axis=3)
+    return lax.all_to_all(windows, "gx", split_axis=2, concat_axis=1, tiled=True)
 
 
 def to_blocks(lines):
     return lax.all_to_all(lines, "gx", split_axis=1, concat_axis=2, tiled=True)
-
-
-def neighbour_lines(line):
-    n_gx, n_gy = lax.axis_size("gx"), lax.axis_size("gy")
-    count = n_gx * n_gy
-
-    def device(c):
-        c = c % count
-        return (c % n_gx) * n_gy + c // n_gx
-
-    from_left = lax.ppermute(line, ("gx", "gy"), [(device(c), device(c + 1)) for c in range(count)])
-    from_right = lax.ppermute(line, ("gx", "gy"), [(device(c + 1), device(c)) for c in range(count)])
-    return from_left, from_right
 
 
 def convolve(columns, conv_weight):
@@ -62,11 +58,10 @@
 
 
 def on_device(field, conv_weight, qkv_weight, out_weight):
-    lines = to_lines(field)
-    planes, length, _, width = lines.shape
-    line = lines.reshape(length, width)
-    from_left, from_right = neighbour_lines(line)
-    stem = convolve(jnp.stack([from_left, line, from_right]), conv_weight)
+    lines = to_lines(padded_columns(field))
+    planes, length, _, _, width = lines.shape
+    columns = jnp.moveaxis(lines.reshape(length, 3, width), 1, 0)
+    stem = convolve(columns, conv_weight)
     normed = normalize(stem)
     attended = attend(normed, qkv_weight)
     projected = jnp.dot(attended, out_weight, preferred_element_type=jnp.float32)

time: 78.6 us -> 75.7 us (0.963)
  starting transfers between devices: 5.12 us -> 8.95 us
  waiting for transfers between devices: 4.45 us -> 0.71 us
  blocking collectives: 55.9 us -> 53 us
    all_to_all x1, blocking collectives: 25.7 us -> 19.8 us  [to_blocks(): return lax.all_to_all(lines, 'gx', split_axis=1, concat_axis=2, tiled=True)]
    ppermute x2, starting transfers between devices: 5.12 us -> 8.95 us  [the longest x1 5 us: padded_columns(): lax.ppermute(block[:, :, :1], 'gy', [((i + 1) % count, i) for i in range(...]
    ppermute x2, waiting for transfers between devices: 4.45 us -> 0.71 us  [the longest x1 0.7 us: padded_columns(): lax.ppermute(block[:, :, :1], 'gy', [((i + 1) % count, i) for i in range(...]
    all_to_all x1, blocking collectives: 30.2 us -> 33.2 us  [to_lines(): lax.all_to_all(windows, 'gx', split_axis=2, concat_axis=1, tiled=True)]
where the time goes in v2:
time: 75.7 us; the launch traced here: 75 us
  blocking collectives  53 us (70%)
  starting transfers between devices  8.95 us (12%)
  matrix products  7.15 us (9%)
  local copies, waits for them, and re-layouts  3.16 us (4%)
  other arithmetic  1.84 us (2%)
    all_to_all x1, blocking collectives, to_lines(): lax.all_to_all(windows, 'gx', split_axis=2, concat_axis=1, tiled=True)  33.2 us
    all_to_all x1, blocking collectives, to_blocks(): return lax.all_to_all(lines, 'gx', split_axis=1, concat_axis=2, tiled=True)  19.8 us
    ppermute x1, starting transfers between devices, padded_columns(): lax.ppermute(block[:, :, :1], 'gy', [((i + 1) % count, i) for i in range(...  5 us
    ppermute x1, starting transfers between devices, padded_columns(): lax.ppermute(block[:, :, -1:], 'gy', [(i, (i + 1) % count) for i in range...  3.95 us
    sub x1, matrix products, attend(): expo = jnp.exp(scores - top)  3.43 us
    dot_general x1, matrix products, attend(): jnp.einsum('hqk,khd->qhd', probs, valued, preferred_element_type=jnp.floa...  2.66 us
    unnamed x14, local copies, waits for them, and re-layouts  2.06 us
    unnamed x6, other arithmetic  1.64 us
  transfers between devices with their start and end apart: 2, of which 1 were waited for; matrix products, arithmetic and copies ran while one was open for 0% of the time, Pallas kernels for 0%

profile of v2, /device:TPU:1, one launch (start us, length us, event | category | flops | bytes accessed | tf_op | source)
XLA Modules:
  0.0 75.0 jit_solution(571464038952185471)
XLA Ops:
  0.0 0.0 copy-start
  0.0 1.0 %copy.36 = bf16[1,8,64,128]{3,1,2,0:T(8,128)(2,1)S(1)} copy(bf16[1,8,64,128]{3,2,1,0:T(8,128)(2,1)} %param.4) | data formatting | bytes 262144 | tf_op args[0]
  1.1 3.9 %collective-permute-start = (bf16[1,8,1,128]{3,1,2,0:T(8,128)(2,1)S(1)}, bf16[1,8,1,128]{3,1,2,0:T(8,128)(2,1)S(1)}, u32[]{:S(2)}, u32[]{:S(2)}) collective-permute-start(bf16[1,8,1,128]{3,1,2,0:T(8,128)(2,1)S(1)} %get-tuple-element.22), channel_id=1, source_target_pairs={{0,1},{1,2},{2,3},{3,4},{4,5},{5,6},{6,7},{7,0},{8,9},{9,10},{10,1... | collective-permute-start | bytes 6152 | tf_op jit(solution)/shard_map/ppermute | solution.py:12
  5.0 5.0 %collective-permute-start.1 = (bf16[1,8,1,128]{3,1,2,0:T(8,128)(2,1)S(1)}, bf16[1,8,1,128]{3,1,2,0:T(8,128)(2,1)S(1)}, u32[]{:S(2)}, u32[]{:S(2)}) collective-permute-start(bf16[1,8,1,128]{3,1,2,0:T(8,128)(2,1)S(1)} %get-tuple-element.23), channel_id=1, source_target_pairs={{1,0},{2,1},{3,2},{4,3},{5,4},{6,5},{7,6},{0,7},{9,8},{10,9},{11,1... | collective-permute-start | bytes 6152 | tf_op jit(solution)/shard_map/ppermute | solution.py:13
  10.0 0.0 collective-permute-done
  10.0 0.7 collective-permute-done.1
  10.8 0.1 pad_maximum_fusion
  10.8 33.2 %all_to_all.33 = bf16[1,8,64,3,128]{4,1,3,0,2:T(8,128)(2,1)S(1)} all-to-all(bf16[1,8,64,3,128]{4,1,3,0,2:T(8,128)(2,1)S(1)} %pad_maximum_fusion), channel_id=1, replica_groups=mesh['gx'=64,'gy'=8] {'gx'}, dimensions={2} | all-to-all | bytes 786432 | tf_op jit(solution)/shard_map/all_to_all | solution.py:20
  44.0 0.1 copy.34
  44.1 0.2 slice_bitcast_fusion
  44.3 0.1 maximum_dynamic-update-slice_fusion.4
  44.4 0.1 maximum_dynamic-update-slice_fusion.3
  44.7 0.0 copy-start.2
  44.7 0.0 copy-done
  44.7 0.5 fusion.21
  45.3 0.1 multiply_reduce_fusion.1
  45.3 0.2 copy-done.2
  45.6 0.3 convolution_convert_fusion
  45.9 3.4 %fusion.22 = (f32[4,512]{1,0:T(4,128)S(1)}, f32[4,512,512]{1,2,0:T(8,128)}) fusion(bf16[512,4,32]{0,2,1:T(8,128)(2,1)S(1)} %bitcast.93, bf16[512,4,32]{0,2,1:T(8,128)(2,1)S(1)} %bitcast.92), kind=kOutput, calls=%fused_computation.55 | convolution fusion | flops 70255104 | bytes 4464640 | tf_op jit(solution)/shard_map/sub | solution.py:54
  49.3 0.0 copy-start.1
  49.3 2.7 %fusion.7 = bf16[4,32,512]{2,1,0:T(8,128)(2,1)S(1)} fusion(bf16[512,4,32]{0,2,1:T(8,128)(2,1)S(1)} %bitcast.91, f32[4,512,512]{1,2,0:T(8,128)} %get-tuple-element.29, f32[4,512]{1,0:T(4,128)S(1)} %get-tuple-element.28), kind=kOutput, calls=%fused_computation.10 | convolution fusion | flops 69271552 | bytes 4464640 | tf_op jit(solution)/shard_map/hqk,khd->qhd/dot_general | solution.py:56
  52.0 0.0 copy-done.1
  52.0 0.2 fusion.8
  52.2 0.2 copy.25
  52.4 0.5 broadcast.26
  52.9 1.4 %reduce = bf16[512,128]{1,0:T(8,128)(2,1)S(1)} reduce(bf16[512,1,1,128]{3,2,1,0:T(2,128)(2,1)S(1)} %bitcast.87, bf16[]{:T(256)} %broadcast.26), dimensions={1,2}, to_apply=%bitcast.65.reduce_sub_computation | reduce | bytes 262146
  54.3 0.1 reshape.55
  54.4 19.8 %all_to_all.34 = bf16[64,2,512]{2,1,0:T(2,128)(2,1)S(1)} all-to-all(bf16[64,2,512]{2,1,0:T(2,128)(2,1)S(1)} %reshape.55), channel_id=1, replica_groups=mesh['gx'=64,'gy'=8] {'gx'}, dimensions={0} | all-to-all | bytes 262144 | tf_op jit(solution)/shard_map/all_to_all | solution.py:24
  74.2 0.1 reshape.56
  74.3 0.7 copy.26
  (14 shorter events, 0.3 us)
Async XLA Ops:
  0.0 44.7 %copy-start = (bf16[3,3,128,128]{3,2,1,0:T(8,128)(2,1)S(1)}, bf16[3,3,128,128]{3,2,1,0:T(8,128)(2,1)}, u32[]{:S(2)}) copy-start(bf16[3,3,128,128]{3,2,1,0:T(8,128)(2,1)} %param.5) | copy-start | bytes 884740
  1.1 9.0 %collective-permute-start = (bf16[1,8,1,128]{3,1,2,0:T(8,128)(2,1)S(1)}, bf16[1,8,1,128]{3,1,2,0:T(8,128)(2,1)S(1)}, u32[]{:S(2)}, u32[]{:S(2)}) collective-permute-start(bf16[1,8,1,128]{3,1,2,0:T(8,128)(2,1)S(1)} %get-tuple-element.22), channel_id=1, source_target_pairs={{0,1},{1,2},{2,3},{3,4},{4,5},{5,6},{6,7},{7,0},{8,9},{9,10},{10,1... | collective-permute-start | bytes 6152 | tf_op jit(solution)/shard_map/ppermute | solution.py:12
  5.0 5.7 %collective-permute-start.1 = (bf16[1,8,1,128]{3,1,2,0:T(8,128)(2,1)S(1)}, bf16[1,8,1,128]{3,1,2,0:T(8,128)(2,1)S(1)}, u32[]{:S(2)}, u32[]{:S(2)}) collective-permute-start(bf16[1,8,1,128]{3,1,2,0:T(8,128)(2,1)S(1)} %get-tuple-element.23), channel_id=1, source_target_pairs={{1,0},{2,1},{3,2},{4,3},{5,4},{6,5},{7,6},{0,7},{9,8},{10,9},{11,1... | collective-permute-start | bytes 6152 | tf_op jit(solution)/shard_map/ppermute | solution.py:13
  44.7 0.9 %copy-start.2 = (bf16[128,384]{1,0:T(8,128)(2,1)S(1)}, bf16[128,384]{1,0:T(8,128)(2,1)}, u32[]{:S(2)}) copy-start(bf16[128,384]{1,0:T(8,128)(2,1)} %param.6) | copy-start | bytes 294916
  49.3 2.7 %copy-start.1 = (bf16[128,128]{1,0:T(8,128)(2,1)S(1)}, bf16[128,128]{1,0:T(8,128)(2,1)}, u32[]{:S(2)}) copy-start(bf16[128,128]{1,0:T(8,128)(2,1)} %param.7) | copy-start | bytes 98308

commit v3 on v2

v3 whole, which is shorter than its diff:
```python
import jax
import jax.numpy as jnp
from jax import lax
from jax.experimental import pallas as pl
from jax.experimental.pallas import tpu as pltpu
from jax.sharding import PartitionSpec as P

HEADS = 4
HEAD = 32


def padded_columns(block):
    count = lax.axis_size("gy")
    left = lax.ppermute(block[:, :, -1:], "gy", [(i, (i + 1) % count) for i in range(count)])
    right = lax.ppermute(block[:, :, :1], "gy", [((i + 1) % count, i) for i in range(count)])
    return jnp.concatenate([left, block, right], axis=2)


def to_lines(padded):
    cols = padded.shape[2] - 2
    windows = jnp.stack([padded[:, :, b : b + cols] for b in range(3)], axis=3)
    return lax.all_to_all(windows, "gx", split_axis=2, concat_axis=1, tiled=True)


def to_blocks(lines):
    return lax.all_to_all(lines, "gx", split_axis=1, concat_axis=2, tiled=True)


def line_kernel(x_ref, cw_ref, qw_ref, ow_ref, o_ref):
    length = x_ref.shape[0]
    width = o_ref.shape[1]
    x = x_ref[...]
    ys = [jnp.dot(x, cw_ref[a], preferred_element_type=jnp.float32) for a in range(3)]
    stem = ys[1] + pltpu.roll(ys[0], 1, 0) + pltpu.roll(ys[2], length - 1, 0)
    mean = jnp.mean(stem, axis=-1, keepdims=True)
    centred = stem - mean
    varia = jnp.mean(centred * centred, axis=-1, keepdims=True)
    normed = (centred / jnp.sqrt(varia + 1e-05)).astype(jnp.bfloat16)
    qkv = jnp.dot(normed, qw_ref[...], preferred_element_type=jnp.float32).astype(jnp.bfloat16)
    scale = 1.0 / jnp.sqrt(jnp.float32(HEAD))
    total = stem
    for h in range(HEADS):
        q = qkv[:, h * HEAD:(h + 1) * HEAD]
        k = qkv[:, width + h * HEAD:width + (h + 1) * HEAD]
        v = qkv[:, 2 * width + h * HEAD:2 * width + (h + 1) * HEAD]
        s = lax.dot_general(q, k, (((1,), (1,)), ((), ())), preferred_element_type=jnp.float32)
        s = s * scale
        m = jnp.max(s, axis=1, keepdims=True)
        e = jnp.exp(s - m)
        l = jnp.sum(e, axis=1, keepdims=True)
        p = (e * (1.0 / l)).astype(jnp.bfloat16)
        o = jnp.dot(p, v, preferred_element_type=jnp.float32).astype(jnp.bfloat16)
        total = total + jnp.dot(o, ow_ref[h * HEAD:(h + 1) * HEAD, :], preferred_element_type=jnp.float32)
    o_ref[...] = total.astype(o_ref.dtype)


def line_block(lines, conv_weight, qkv_weight, out_weight):
    length = lines.shape[0]; width = out_weight.shape[1]
    cw = conv_weight.reshape(3, 3 * width, width)
    vm = pl.BlockSpec(memory_space=pltpu.VMEM)
    return pl.pallas_call(line_kernel, out_shape=jax.ShapeDtypeStruct((length, width), jnp.bfloat16),
        in_specs=[vm]*4, out_specs=vm)(lines, cw, qkv_weight, out_weight)


def on_device(field, conv_weight, qkv_weight, out_weight):
    lines = to_lines(padded_columns(field))
    planes, length, _, taps, width = lines.shape
    result = line_block(lines.reshape(length, taps * width), conv_weight, qkv_weight, out_weight)
    return to_blocks(result.reshape(planes, length, 1, width))


def solution(mesh):
    placed = (P(None, "gx", "gy", None), P(), P(), P())
    return jax.shard_map(
        on_device, mesh=mesh, in_specs=placed, out_specs=P(None, "gx", "gy", None), check_vma=False
    )
```

time: 75.7 us -> 74.5 us (0.984)
  matrix products: 7.15 us -> 0 us
  Pallas kernels: 0 us -> 6.08 us
    pallas_call x0 -> x1, Pallas kernels: none -> 6.08 us  [line_block(): pl.pallas_call(line_kernel, out_shape=jax.ShapeDtypeStruct((length, width...]
    dot_general x4 -> x0, matrix products: 3.72 us -> none  [the longest x1 2.66 us: attend(): jnp.einsum('hqk,khd->qhd', probs, valued, preferred_element_type=jnp.floa...]
    sub x1 -> x0, matrix products: 3.43 us -> none  [attend(): expo = jnp.exp(scores - top)]
    reshape x1, local copies, waits for them, and re-layouts: 0.16 us -> 1.11 us  [on_device(): return to_blocks(result.reshape(planes, length, 1, width))]
    unnamed x14 -> x5, local copies, waits for them, and re-layouts: 2.06 us -> 1.68 us
    unnamed x6 -> x1, other arithmetic: 1.64 us -> 1.41 us
where the time goes in v3:
time: 74.5 us; the launch traced here: 73.9 us
  blocking collectives  53.1 us (71%)
  starting transfers between devices  8.95 us (12%)
  Pallas kernels  6.08 us (8%)
  local copies, waits for them, and re-layouts  3.47 us (5%)
  other arithmetic  1.51 us (2%)
    all_to_all x1, blocking collectives, to_lines(): lax.all_to_all(windows, 'gx', split_axis=2, concat_axis=1, tiled=True)  33.3 us
    all_to_all x1, blocking collectives, to_blocks(): return lax.all_to_all(lines, 'gx', split_axis=1, concat_axis=2, tiled=True)  19.8 us
    pallas_call x1, Pallas kernels, line_block(): pl.pallas_call(line_kernel, out_shape=jax.ShapeDtypeStruct((length, width...  6.08 us
    ppermute x1, starting transfers between devices, padded_columns(): lax.ppermute(block[:, :, :1], 'gy', [((i + 1) % count, i) for i in range(...  5 us
    ppermute x1, starting transfers between devices, padded_columns(): lax.ppermute(block[:, :, -1:], 'gy', [(i, (i + 1) % count) for i in range...  3.95 us
    unnamed x5, local copies, waits for them, and re-layouts  1.68 us
  transfers between devices with their start and end apart: 2, of which 1 were waited for; matrix products, arithmetic and copies ran while one was open for 0% of the time, Pallas kernels for 0%

profile of v3, /device:TPU:1, one launch (start us, length us, event | category | flops | bytes accessed | tf_op | source)
XLA Modules:
  0.0 73.9 jit_solution(10721321711664603043)
XLA Ops:
  0.0 1.0 %copy.27 = bf16[1,8,64,128]{3,1,2,0:T(8,128)(2,1)S(1)} copy(bf16[1,8,64,128]{3,2,1,0:T(8,128)(2,1)} %param.4) | data formatting | bytes 262144 | tf_op args[0]
  1.0 3.9 %collective-permute-start = (bf16[1,8,1,128]{3,1,2,0:T(8,128)(2,1)S(1)}, bf16[1,8,1,128]{3,1,2,0:T(8,128)(2,1)S(1)}, u32[]{:S(2)}, u32[]{:S(2)}) collective-permute-start(bf16[1,8,1,128]{3,1,2,0:T(8,128)(2,1)S(1)} %get-tuple-element.7), channel_id=1, source_target_pairs={{0,1},{1,2},{2,3},{3,4},{4,5},{5,6},{6,7},{7,0},{8,9},{9,10},{10,1... | collective-permute-start | bytes 6152 | tf_op jit(solution)/shard_map/ppermute | solution.py:14
  5.0 5.0 %collective-permute-start.1 = (bf16[1,8,1,128]{3,1,2,0:T(8,128)(2,1)S(1)}, bf16[1,8,1,128]{3,1,2,0:T(8,128)(2,1)S(1)}, u32[]{:S(2)}, u32[]{:S(2)}) collective-permute-start(bf16[1,8,1,128]{3,1,2,0:T(8,128)(2,1)S(1)} %get-tuple-element.8), channel_id=1, source_target_pairs={{1,0},{2,1},{3,2},{4,3},{5,4},{6,5},{7,6},{0,7},{9,8},{10,9},{11,1... | collective-permute-start | bytes 6152 | tf_op jit(solution)/shard_map/ppermute | solution.py:15
  10.0 0.0 collective-permute-done
  10.0 0.7 collective-permute-done.1
  10.7 0.1 pad_maximum_fusion
  10.8 33.3 %all_to_all.33 = bf16[1,8,64,3,128]{4,1,3,0,2:T(8,128)(2,1)} all-to-all(bf16[1,8,64,3,128]{4,1,3,0,2:T(8,128)(2,1)S(1)} %pad_maximum_fusion), channel_id=1, replica_groups=mesh['gx'=64,'gy'=8] {'gx'}, dimensions={2} | all-to-all | bytes 786432 | tf_op jit(solution)/shard_map/all_to_all | solution.py:22
  44.1 6.1 %shard_map.46 = bf16[512,128]{1,0:T(8,128)(2,1)} custom-call(bf16[512,384]{1,0:T(8,128)(2,1)} %bitcast.25, bf16[3,384,128]{2,1,0:T(8,128)(2,1)} %bitcast.31, bf16[128,384]{1,0:T(8,128)(2,1)} %qw_ref.1, bf16[128,128]{1,0:T(8,128)(2,1)} %ow_ref.1), custom_call_target="tpu_custom_call" | custom-call | tf_op jit(solution)/shard_map/pallas_call | solution.py:61
  50.2 1.1 %copy.28 = bf16[1,512,1,128]{3,2,0,1:T(2,128)(2,1)S(1)} copy(bf16[1,512,1,128]{3,1,2,0:T(8,128)(2,1)} %bitcast.30) | data formatting | bytes 262144 | tf_op jit(solution)/shard_map/reshape | solution.py:69
  51.3 0.5 broadcast
  51.8 1.4 %reduce = bf16[512,128]{1,0:T(8,128)(2,1)S(1)} reduce(bf16[512,1,1,128]{3,2,1,0:T(2,128)(2,1)S(1)} %bitcast.27, bf16[]{:T(256)} %broadcast), dimensions={1,2}, to_apply=%bitcast.24.reduce_sub_computation | reduce | bytes 262146
  53.2 0.1 reshape.13
  53.3 19.8 %all_to_all.34 = bf16[64,2,512]{2,1,0:T(2,128)(2,1)S(1)} all-to-all(bf16[64,2,512]{2,1,0:T(2,128)(2,1)S(1)} %reshape.13), channel_id=1, replica_groups=mesh['gx'=64,'gy'=8] {'gx'}, dimensions={0} | all-to-all | bytes 262144 | tf_op jit(solution)/shard_map/all_to_all | solution.py:26
  73.1 0.1 reshape.14
  73.2 0.7 copy.20
  (3 shorter events, 0.0 us)
Async XLA Ops:
  1.0 9.0 %collective-permute-start = (bf16[1,8,1,128]{3,1,2,0:T(8,128)(2,1)S(1)}, bf16[1,8,1,128]{3,1,2,0:T(8,128)(2,1)S(1)}, u32[]{:S(2)}, u32[]{:S(2)}) collective-permute-start(bf16[1,8,1,128]{3,1,2,0:T(8,128)(2,1)S(1)} %get-tuple-element.7), channel_id=1, source_target_pairs={{0,1},{1,2},{2,3},{3,4},{4,5},{5,6},{6,7},{7,0},{8,9},{9,10},{10,1... | collective-permute-start | bytes 6152 | tf_op jit(solution)/shard_map/ppermute | solution.py:14
  5.0 5.7 %collective-permute-start.1 = (bf16[1,8,1,128]{3,1,2,0:T(8,128)(2,1)S(1)}, bf16[1,8,1,128]{3,1,2,0:T(8,128)(2,1)S(1)}, u32[]{:S(2)}, u32[]{:S(2)}) collective-permute-start(bf16[1,8,1,128]{3,1,2,0:T(8,128)(2,1)S(1)} %get-tuple-element.8), channel_id=1, source_target_pairs={{1,0},{2,1},{3,2},{4,3},{5,4},{6,5},{7,6},{0,7},{9,8},{10,9},{11,1... | collective-permute-start | bytes 6152 | tf_op jit(solution)/shard_map/ppermute | solution.py:15

commit v4 on v3

--- a/solution.py
+++ b/solution.py
@@ -22,8 +22,10 @@
     return lax.all_to_all(windows, "gx", split_axis=2, concat_axis=1, tiled=True)
 
 
-def to_blocks(lines):
-    return lax.all_to_all(lines, "gx", split_axis=1, concat_axis=2, tiled=True)
+def to_blocks(result, rows):
+    length, width = result.shape
+    chunks = result.reshape(length // rows, rows, 1, width)
+    return lax.all_to_all(chunks, "gx", split_axis=0, concat_axis=2, tiled=True)
 
 
 def line_kernel(x_ref, cw_ref, qw_ref, ow_ref, o_ref):
@@ -66,7 +68,7 @@
     lines = to_lines(padded_columns(field))
     planes, length, _, taps, width = lines.shape
     result = line_block(lines.reshape(length, taps * width), conv_weight, qkv_weight, out_weight)
-    return to_blocks(result.reshape(planes, length, 1, width))
+    return to_blocks(result, field.shape[1])
 
 
 def solution(mesh):

time: 74.5 us -> 71.5 us (0.960)
  local copies, waits for them, and re-layouts: 3.47 us -> 1.67 us
  other arithmetic: 1.51 us -> 0.1 us
    unnamed x1 -> x0, other arithmetic: 1.41 us -> none
    reshape x1 -> x0, local copies, waits for them, and re-layouts: 1.11 us -> none  [on_device(): return to_blocks(result.reshape(planes, length, 1, width))]
    unnamed x5 -> x1, local copies, waits for them, and re-layouts: 1.68 us -> 0.99 us
where the time goes in v4:
time: 71.5 us; the launch traced here: 70.9 us
  blocking collectives  53.3 us (75%)
  starting transfers between devices  8.95 us (13%)
  Pallas kernels  6.08 us (9%)
  local copies, waits for them, and re-layouts  1.67 us (2%)
    all_to_all x1, blocking collectives, to_lines(): lax.all_to_all(windows, 'gx', split_axis=2, concat_axis=1, tiled=True)  33.3 us
    all_to_all x1, blocking collectives, to_blocks(): return lax.all_to_all(chunks, 'gx', split_axis=0, concat_axis=2, tiled=True)  20 us
    pallas_call x1, Pallas kernels, line_block(): pl.pallas_call(line_kernel, out_shape=jax.ShapeDtypeStruct((length, width...  6.08 us
    ppermute x1, starting transfers between devices, padded_columns(): lax.ppermute(block[:, :, :1], 'gy', [((i + 1) % count, i) for i in range(...  5 us
    ppermute x1, starting transfers between devices, padded_columns(): lax.ppermute(block[:, :, -1:], 'gy', [(i, (i + 1) % count) for i in range...  3.95 us
  transfers between devices with their start and end apart: 2, of which 1 were waited for; matrix products, arithmetic and copies ran while one was open for 0% of the time, Pallas kernels for 0%

profile of v4, /device:TPU:1, one launch (start us, length us, event | category | flops | bytes accessed | tf_op | source)
XLA Modules:
  0.0 70.9 jit_solution(6047767474441720208)
XLA Ops:
  0.0 1.0 %copy.16 = bf16[1,8,64,128]{3,1,2,0:T(8,128)(2,1)S(1)} copy(bf16[1,8,64,128]{3,2,1,0:T(8,128)(2,1)} %param.4) | data formatting | bytes 262144 | tf_op args[0]
  1.0 3.9 %collective-permute-start = (bf16[1,8,1,128]{3,1,2,0:T(8,128)(2,1)S(1)}, bf16[1,8,1,128]{3,1,2,0:T(8,128)(2,1)S(1)}, u32[]{:S(2)}, u32[]{:S(2)}) collective-permute-start(bf16[1,8,1,128]{3,1,2,0:T(8,128)(2,1)S(1)} %get-tuple-element.7), channel_id=1, source_target_pairs={{0,1},{1,2},{2,3},{3,4},{4,5},{5,6},{6,7},{7,0},{8,9},{9,10},{10,1... | collective-permute-start | bytes 6152 | tf_op jit(solution)/shard_map/ppermute | solution.py:14
  5.0 5.0 %collective-permute-start.1 = (bf16[1,8,1,128]{3,1,2,0:T(8,128)(2,1)S(1)}, bf16[1,8,1,128]{3,1,2,0:T(8,128)(2,1)S(1)}, u32[]{:S(2)}, u32[]{:S(2)}) collective-permute-start(bf16[1,8,1,128]{3,1,2,0:T(8,128)(2,1)S(1)} %get-tuple-element.8), channel_id=1, source_target_pairs={{1,0},{2,1},{3,2},{4,3},{5,4},{6,5},{7,6},{0,7},{9,8},{10,9},{11,1... | collective-permute-start | bytes 6152 | tf_op jit(solution)/shard_map/ppermute | solution.py:15
  10.0 0.0 collective-permute-done
  10.0 0.7 collective-permute-done.1
  10.7 0.1 pad_maximum_fusion
  10.8 33.3 %all_to_all.33 = bf16[1,8,64,3,128]{4,1,3,0,2:T(8,128)(2,1)} all-to-all(bf16[1,8,64,3,128]{4,1,3,0,2:T(8,128)(2,1)S(1)} %pad_maximum_fusion), channel_id=1, replica_groups=mesh['gx'=64,'gy'=8] {'gx'}, dimensions={2} | all-to-all | bytes 786432 | tf_op jit(solution)/shard_map/all_to_all | solution.py:22
  44.1 6.1 %shard_map.46 = bf16[512,128]{1,0:T(8,128)(2,1)} custom-call(bf16[512,384]{1,0:T(8,128)(2,1)} %bitcast.21, bf16[3,384,128]{2,1,0:T(8,128)(2,1)} %bitcast.25, bf16[128,384]{1,0:T(8,128)(2,1)} %qw_ref.1, bf16[128,128]{1,0:T(8,128)(2,1)} %ow_ref.1), custom_call_target="tpu_custom_call" | custom-call | tf_op jit(solution)/shard_map/pallas_call | solution.py:63
  50.2 20.0 %all_to_all.34 = bf16[64,8,1,128]{3,1,2,0:T(8,128)(2,1)S(1)} all-to-all(bf16[64,8,1,128]{3,1,2,0:T(8,128)(2,1)} %bitcast.24), channel_id=1, replica_groups=mesh['gx'=64,'gy'=8] {'gx'}, dimensions={0} | all-to-all | bytes 262144 | tf_op jit(solution)/shard_map/all_to_all | solution.py:28
  70.2 0.7 copy.13
  (2 shorter events, 0.0 us)
Async XLA Ops:
  1.0 9.0 %collective-permute-start = (bf16[1,8,1,128]{3,1,2,0:T(8,128)(2,1)S(1)}, bf16[1,8,1,128]{3,1,2,0:T(8,128)(2,1)S(1)}, u32[]{:S(2)}, u32[]{:S(2)}) collective-permute-start(bf16[1,8,1,128]{3,1,2,0:T(8,128)(2,1)S(1)} %get-tuple-element.7), channel_id=1, source_target_pairs={{0,1},{1,2},{2,3},{3,4},{4,5},{5,6},{6,7},{7,0},{8,9},{9,10},{10,1... | collective-permute-start | bytes 6152 | tf_op jit(solution)/shard_map/ppermute | solution.py:14
  5.0 5.7 %collective-permute-start.1 = (bf16[1,8,1,128]{3,1,2,0:T(8,128)(2,1)S(1)}, bf16[1,8,1,128]{3,1,2,0:T(8,128)(2,1)S(1)}, u32[]{:S(2)}, u32[]{:S(2)}) collective-permute-start(bf16[1,8,1,128]{3,1,2,0:T(8,128)(2,1)S(1)} %get-tuple-element.8), channel_id=1, source_target_pairs={{1,0},{2,1},{3,2},{4,3},{5,4},{6,5},{7,6},{0,7},{9,8},{10,9},{11,1... | collective-permute-start | bytes 6152 | tf_op jit(solution)/shard_map/ppermute | solution.py:15

commit v5 on v4

--- a/solution.py
+++ b/solution.py
@@ -32,27 +32,31 @@
     length = x_ref.shape[0]
     width = o_ref.shape[1]
     x = x_ref[...]
-    ys = [jnp.dot(x, cw_ref[a], preferred_element_type=jnp.float32) for a in range(3)]
-    stem = ys[1] + pltpu.roll(ys[0], 1, 0) + pltpu.roll(ys[2], length - 1, 0)
+    taps = jnp.dot(x, jnp.concatenate([cw_ref[a] for a in range(3)], axis=1),
+                   preferred_element_type=jnp.float32)
+    stem = (taps[:, width:2 * width] + pltpu.roll(taps[:, :width], 1, 0)
+            + pltpu.roll(taps[:, 2 * width:], length - 1, 0))
     mean = jnp.mean(stem, axis=-1, keepdims=True)
     centred = stem - mean
     varia = jnp.mean(centred * centred, axis=-1, keepdims=True)
     normed = (centred / jnp.sqrt(varia + 1e-05)).astype(jnp.bfloat16)
     qkv = jnp.dot(normed, qw_ref[...], preferred_element_type=jnp.float32).astype(jnp.bfloat16)
+    query, keyed, valued = qkv[:, :width], qkv[:, width:2 * width], qkv[:, 2 * width:]
+    head_of = lax.broadcasted_iota(jnp.int32, (length, width), 1) // HEAD
+    zero = jnp.zeros_like(keyed)
+    keys = jnp.concatenate([jnp.where(head_of == h, keyed, zero) for h in range(HEADS)], axis=0)
+    values = jnp.concatenate([jnp.where(head_of == h, valued, zero) for h in range(HEADS)], axis=0)
+    scores = lax.dot_general(query, keys, (((1,), (1,)), ((), ())), preferred_element_type=jnp.float32)
     scale = 1.0 / jnp.sqrt(jnp.float32(HEAD))
-    total = stem
+    weights, inverse = [], jnp.zeros((length, width), jnp.float32)
     for h in range(HEADS):
-        q = qkv[:, h * HEAD:(h + 1) * HEAD]
-        k = qkv[:, width + h * HEAD:width + (h + 1) * HEAD]
-        v = qkv[:, 2 * width + h * HEAD:2 * width + (h + 1) * HEAD]
-        s = lax.dot_general(q, k, (((1,), (1,)), ((), ())), preferred_element_type=jnp.float32)
-        s = s * scale
-        m = jnp.max(s, axis=1, keepdims=True)
-        e = jnp.exp(s - m)
-        l = jnp.sum(e, axis=1, keepdims=True)
-        p = (e * (1.0 / l)).astype(jnp.bfloat16)
-        o = jnp.dot(p, v, preferred_element_type=jnp.float32).astype(jnp.bfloat16)
-        total = total + jnp.dot(o, ow_ref[h * HEAD:(h + 1) * HEAD, :], preferred_element_type=jnp.float32)
+        s = scores[:, h * length:(h + 1) * length] * scale
+        e = jnp.exp(s - jnp.max(s, axis=1, keepdims=True))
+        weights.append(e.astype(jnp.bfloat16))
+        inverse = jnp.where(head_of == h, 1.0 / jnp.sum(e, axis=1, keepdims=True), inverse)
+    mixed = jnp.dot(jnp.concatenate(weights, axis=1), values, preferred_element_type=jnp.float32)
+    attended = (mixed * inverse).astype(jnp.bfloat16)
+    total = stem + jnp.dot(attended, ow_ref[...], preferred_element_type=jnp.float32)
     o_ref[...] = total.astype(o_ref.dtype)
 
 

time: 71.5 us -> 70.2 us (0.982)
  Pallas kernels: 6.08 us -> 4.74 us
    pallas_call x1, Pallas kernels: 6.08 us -> 4.74 us  [line_block(): pl.pallas_call(line_kernel, out_shape=jax.ShapeDtypeStruct((length, width...]
where the time goes in v5:
time: 70.2 us; the launch traced here: 69.5 us
  blocking collectives  53.3 us (76%)
  starting transfers between devices  8.95 us (13%)
  Pallas kernels  4.74 us (7%)
  local copies, waits for them, and re-layouts  1.67 us (2%)
  waiting for transfers between devices  0.71 us (1%)
    all_to_all x1, blocking collectives, to_lines(): lax.all_to_all(windows, 'gx', split_axis=2, concat_axis=1, tiled=True)  33.3 us
    all_to_all x1, blocking collectives, to_blocks(): return lax.all_to_all(chunks, 'gx', split_axis=0, concat_axis=2, tiled=True)  20 us
    ppermute x1, starting transfers between devices, padded_columns(): lax.ppermute(block[:, :, :1], 'gy', [((i + 1) % count, i) for i in range(...  5 us
    pallas_call x1, Pallas kernels, line_block(): pl.pallas_call(line_kernel, out_shape=jax.ShapeDtypeStruct((length, width...  4.74 us
    ppermute x1, starting transfers between devices, padded_columns(): lax.ppermute(block[:, :, -1:], 'gy', [(i, (i + 1) % count) for i in range...  3.95 us
  transfers between devices with their start and end apart: 2, of which 1 were waited for; matrix products, arithmetic and copies ran while one was open for 0% of the time, Pallas kernels for 0%

profile of v5, /device:TPU:1, one launch (start us, length us, event | category | flops | bytes accessed | tf_op | source)
XLA Modules:
  0.0 69.5 jit_solution(11189755915268771205)
XLA Ops:
  0.0 1.0 %copy.16 = bf16[1,8,64,128]{3,1,2,0:T(8,128)(2,1)S(1)} copy(bf16[1,8,64,128]{3,2,1,0:T(8,128)(2,1)} %param.4) | data formatting | bytes 262144 | tf_op args[0]
  1.0 3.9 %collective-permute-start = (bf16[1,8,1,128]{3,1,2,0:T(8,128)(2,1)S(1)}, bf16[1,8,1,128]{3,1,2,0:T(8,128)(2,1)S(1)}, u32[]{:S(2)}, u32[]{:S(2)}) collective-permute-start(bf16[1,8,1,128]{3,1,2,0:T(8,128)(2,1)S(1)} %get-tuple-element.7), channel_id=1, source_target_pairs={{0,1},{1,2},{2,3},{3,4},{4,5},{5,6},{6,7},{7,0},{8,9},{9,10},{10,1... | collective-permute-start | bytes 6152 | tf_op jit(solution)/shard_map/ppermute | solution.py:14
  5.0 5.0 %collective-permute-start.1 = (bf16[1,8,1,128]{3,1,2,0:T(8,128)(2,1)S(1)}, bf16[1,8,1,128]{3,1,2,0:T(8,128)(2,1)S(1)}, u32[]{:S(2)}, u32[]{:S(2)}) collective-permute-start(bf16[1,8,1,128]{3,1,2,0:T(8,128)(2,1)S(1)} %get-tuple-element.8), channel_id=1, source_target_pairs={{1,0},{2,1},{3,2},{4,3},{5,4},{6,5},{7,6},{0,7},{9,8},{10,9},{11,1... | collective-permute-start | bytes 6152 | tf_op jit(solution)/shard_map/ppermute | solution.py:15
  10.0 0.0 collective-permute-done
  10.0 0.7 %collective-permute-done.1 = bf16[1,8,1,128]{3,1,2,0:T(8,128)(2,1)S(1)} collective-permute-done((bf16[1,8,1,128]{3,1,2,0:T(8,128)(2,1)S(1)}, bf16[1,8,1,128]{3,1,2,0:T(8,128)(2,1)S(1)}, u32[]{:S(2)}, u32[]{:S(2)}) %collective-permute-start.1) | collective-permute-done | bytes 2080 | tf_op jit(solution)/shard_map/ppermute | solution.py:15
  10.7 0.1 pad_maximum_fusion
  10.8 33.3 %all_to_all.33 = bf16[1,8,64,3,128]{4,1,3,0,2:T(8,128)(2,1)} all-to-all(bf16[1,8,64,3,128]{4,1,3,0,2:T(8,128)(2,1)S(1)} %pad_maximum_fusion), channel_id=1, replica_groups=mesh['gx'=64,'gy'=8] {'gx'}, dimensions={2} | all-to-all | bytes 786432 | tf_op jit(solution)/shard_map/all_to_all | solution.py:22
  44.1 4.7 %shard_map.46 = bf16[512,128]{1,0:T(8,128)(2,1)} custom-call(bf16[512,384]{1,0:T(8,128)(2,1)} %bitcast.21, bf16[3,384,128]{2,1,0:T(8,128)(2,1)} %bitcast.25, bf16[128,384]{1,0:T(8,128)(2,1)} %qw_ref.1, bf16[128,128]{1,0:T(8,128)(2,1)} %ow_ref.1), custom_call_target="tpu_custom_call" | custom-call | tf_op jit(solution)/shard_map/pallas_call | solution.py:67
  48.8 20.0 %all_to_all.34 = bf16[64,8,1,128]{3,1,2,0:T(8,128)(2,1)S(1)} all-to-all(bf16[64,8,1,128]{3,1,2,0:T(8,128)(2,1)} %bitcast.24), channel_id=1, replica_groups=mesh['gx'=64,'gy'=8] {'gx'}, dimensions={0} | all-to-all | bytes 262144 | tf_op jit(solution)/shard_map/all_to_all | solution.py:28
  68.8 0.7 copy.13
  (2 shorter events, 0.0 us)
Async XLA Ops:
  1.0 9.0 %collective-permute-start = (bf16[1,8,1,128]{3,1,2,0:T(8,128)(2,1)S(1)}, bf16[1,8,1,128]{3,1,2,0:T(8,128)(2,1)S(1)}, u32[]{:S(2)}, u32[]{:S(2)}) collective-permute-start(bf16[1,8,1,128]{3,1,2,0:T(8,128)(2,1)S(1)} %get-tuple-element.7), channel_id=1, source_target_pairs={{0,1},{1,2},{2,3},{3,4},{4,5},{5,6},{6,7},{7,0},{8,9},{9,10},{10,1... | collective-permute-start | bytes 6152 | tf_op jit(solution)/shard_map/ppermute | solution.py:14
  5.0 5.7 %collective-permute-start.1 = (bf16[1,8,1,128]{3,1,2,0:T(8,128)(2,1)S(1)}, bf16[1,8,1,128]{3,1,2,0:T(8,128)(2,1)S(1)}, u32[]{:S(2)}, u32[]{:S(2)}) collective-permute-start(bf16[1,8,1,128]{3,1,2,0:T(8,128)(2,1)S(1)} %get-tuple-element.8), channel_id=1, source_target_pairs={{1,0},{2,1},{3,2},{4,3},{5,4},{6,5},{7,6},{0,7},{9,8},{10,9},{11,1... | collective-permute-start | bytes 6152 | tf_op jit(solution)/shard_map/ppermute | solution.py:15

commit v6 on v5

--- a/solution.py
+++ b/solution.py
@@ -11,8 +11,9 @@
 
 def padded_columns(block):
     count = lax.axis_size("gy")
-    left = lax.ppermute(block[:, :, -1:], "gy", [(i, (i + 1) % count) for i in range(count)])
-    right = lax.ppermute(block[:, :, :1], "gy", [((i + 1) % count, i) for i in range(count)])
+    rims = lax.optimization_barrier(block)
+    left = lax.ppermute(rims[:, :, -1:], "gy", [(i, (i + 1) % count) for i in range(count)])
+    right = lax.ppermute(rims[:, :, :1], "gy", [((i + 1) % count, i) for i in range(count)])
     return jnp.concatenate([left, block, right], axis=2)
 
 

time: 70.2 us -> 73.1 us (1.041)
  waiting for transfers between devices: 0.71 us -> 3.5 us
  local copies, waits for them, and re-layouts: 1.67 us -> 2.42 us
    ppermute x2, waiting for transfers between devices: 0.71 us -> 3.5 us  [the longest x1 3.5 us: padded_columns(): lax.ppermute(rims[:, :, -1:], 'gy', [(i, (i + 1) % count) for i in range(...]
    slice x1, local copies, waits for them, and re-layouts: 0.01 us -> 0.74 us  [padded_columns(): rims[:, :, -1:]]
  transfers between devices with their start and end apart: 2 -> 2, of which waited for: 1 -> 1; matrix products, arithmetic and copies ran while one was open for 0% -> 1% of each run, Pallas kernels for 0% -> 0%
where the time goes in v6:
time: 73.1 us; the launch traced here: 72.8 us
  blocking collectives  53 us (73%)
  starting transfers between devices  8.95 us (12%)
  Pallas kernels  4.74 us (6%)
  waiting for transfers between devices  3.5 us (5%)
  local copies, waits for them, and re-layouts  2.42 us (3%)
    all_to_all x1, blocking collectives, to_lines(): lax.all_to_all(windows, 'gx', split_axis=2, concat_axis=1, tiled=True)  33.2 us
    all_to_all x1, blocking collectives, to_blocks(): return lax.all_to_all(chunks, 'gx', split_axis=0, concat_axis=2, tiled=True)  19.8 us
    ppermute x1, starting transfers between devices, padded_columns(): lax.ppermute(rims[:, :, :1], 'gy', [((i + 1) % count, i) for i in range(c...  7.02 us
    pallas_call x1, Pallas kernels, line_block(): pl.pallas_call(line_kernel, out_shape=jax.ShapeDtypeStruct((length, width...  4.74 us
    ppermute x1, waiting for transfers between devices, padded_columns(): lax.ppermute(rims[:, :, -1:], 'gy', [(i, (i + 1) % count) for i in range(...  3.5 us
    ppermute x1, starting transfers between devices, padded_columns(): lax.ppermute(rims[:, :, -1:], 'gy', [(i, (i + 1) % count) for i in range(...  1.92 us
  transfers between devices with their start and end apart: 2, of which 1 were waited for; matrix products, arithmetic and copies ran while one was open for 1% of the time, Pallas kernels for 0%

profile of v6, /device:TPU:1, one launch (start us, length us, event | category | flops | bytes accessed | tf_op | source)
XLA Modules:
  0.0 72.8 jit_solution(12036517790889665406)
XLA Ops:
  0.0 0.7 %fusion.2 = (bf16[1,8,1,128]{3,2,1,0:T(2,128)(2,1)S(1)}, bf16[1,8,1,128]{3,2,1,0:T(2,128)(2,1)S(1)}) fusion(bf16[1,8,64,128]{3,2,1,0:T(8,128)(2,1)} %param.4), kind=kLoop, calls=%fused_computation.6 | loop fusion | bytes 8192 | tf_op jit(solution)/shard_map/slice | solution.py:15
  0.8 7.0 %collective-permute-start.1 = (bf16[1,8,1,128]{3,1,2,0:T(8,128)(2,1)S(1)}, bf16[1,8,1,128]{3,1,2,0:T(8,128)(2,1)S(1)}, u32[]{:S(2)}, u32[]{:S(2)}) collective-permute-start(bf16[1,8,1,128]{3,1,2,0:T(8,128)(2,1)S(1)} %copy.15), channel_id=1, source_target_pairs={{1,0},{2,1},{3,2},{4,3},{5,4},{6,5},{7,6},{0,7},{9,8},{10,9},{11,1... | collective-permute-start | bytes 6152 | tf_op jit(solution)/shard_map/ppermute | solution.py:16
  7.8 1.9 %collective-permute-start = (bf16[1,8,1,128]{3,1,2,0:T(8,128)(2,1)S(1)}, bf16[1,8,1,128]{3,1,2,0:T(8,128)(2,1)S(1)}, u32[]{:S(2)}, u32[]{:S(2)}) collective-permute-start(bf16[1,8,1,128]{3,1,2,0:T(8,128)(2,1)S(1)} %copy.14), channel_id=1, source_target_pairs={{0,1},{1,2},{2,3},{3,4},{4,5},{5,6},{6,7},{7,0},{8,9},{9,10},{10,1... | collective-permute-start | bytes 6152 | tf_op jit(solution)/shard_map/ppermute | solution.py:15
  9.7 1.0 %copy.18 = bf16[1,8,64,128]{3,1,2,0:T(8,128)(2,1)S(1)} copy(bf16[1,8,64,128]{3,2,1,0:T(8,128)(2,1)} %param.4) | data formatting | bytes 262144 | tf_op args[0]
  10.7 0.0 collective-permute-done.1
  10.7 3.5 %collective-permute-done = bf16[1,8,1,128]{3,1,2,0:T(8,128)(2,1)S(1)} collective-permute-done((bf16[1,8,1,128]{3,1,2,0:T(8,128)(2,1)S(1)}, bf16[1,8,1,128]{3,1,2,0:T(8,128)(2,1)S(1)}, u32[]{:S(2)}, u32[]{:S(2)}) %collective-permute-start) | collective-permute-done | bytes 2080 | tf_op jit(solution)/shard_map/ppermute | solution.py:15
  14.3 0.1 pad_maximum_fusion
  14.4 33.2 %all_to_all.33 = bf16[1,8,64,3,128]{4,1,3,0,2:T(8,128)(2,1)} all-to-all(bf16[1,8,64,3,128]{4,1,3,0,2:T(8,128)(2,1)S(1)} %pad_maximum_fusion), channel_id=1, replica_groups=mesh['gx'=64,'gy'=8] {'gx'}, dimensions={2} | all-to-all | bytes 786432 | tf_op jit(solution)/shard_map/all_to_all | solution.py:23
  47.5 4.7 %shard_map.46 = bf16[512,128]{1,0:T(8,128)(2,1)} custom-call(bf16[512,384]{1,0:T(8,128)(2,1)} %bitcast.21, bf16[3,384,128]{2,1,0:T(8,128)(2,1)} %bitcast.25, bf16[128,384]{1,0:T(8,128)(2,1)} %qw_ref.1, bf16[128,128]{1,0:T(8,128)(2,1)} %ow_ref.1), custom_call_target="tpu_custom_call" | custom-call | tf_op jit(solution)/shard_map/pallas_call | solution.py:68
  52.3 19.8 %all_to_all.34 = bf16[64,8,1,128]{3,1,2,0:T(8,128)(2,1)S(1)} all-to-all(bf16[64,8,1,128]{3,1,2,0:T(8,128)(2,1)} %bitcast.24), channel_id=1, replica_groups=mesh['gx'=64,'gy'=8] {'gx'}, dimensions={0} | all-to-all | bytes 262144 | tf_op jit(solution)/shard_map/all_to_all | solution.py:29
  72.1 0.7 copy.13
  (3 shorter events, 0.0 us)
Async XLA Ops:
  0.8 10.0 %collective-permute-start.1 = (bf16[1,8,1,128]{3,1,2,0:T(8,128)(2,1)S(1)}, bf16[1,8,1,128]{3,1,2,0:T(8,128)(2,1)S(1)}, u32[]{:S(2)}, u32[]{:S(2)}) collective-permute-start(bf16[1,8,1,128]{3,1,2,0:T(8,128)(2,1)S(1)} %copy.15), channel_id=1, source_target_pairs={{1,0},{2,1},{3,2},{4,3},{5,4},{6,5},{7,6},{0,7},{9,8},{10,9},{11,1... | collective-permute-start | bytes 6152 | tf_op jit(solution)/shard_map/ppermute | solution.py:16
  7.8 6.4 %collective-permute-start = (bf16[1,8,1,128]{3,1,2,0:T(8,128)(2,1)S(1)}, bf16[1,8,1,128]{3,1,2,0:T(8,128)(2,1)S(1)}, u32[]{:S(2)}, u32[]{:S(2)}) collective-permute-start(bf16[1,8,1,128]{3,1,2,0:T(8,128)(2,1)S(1)} %copy.14), channel_id=1, source_target_pairs={{0,1},{1,2},{2,3},{3,4},{4,5},{5,6},{6,7},{7,0},{8,9},{9,10},{10,1... | collective-permute-start | bytes 6152 | tf_op jit(solution)/shard_map/ppermute | solution.py:15

commit v7 on v5

--- a/solution.py
+++ b/solution.py
@@ -9,23 +9,38 @@
 HEAD = 32
 
 
-def padded_columns(block):
-    count = lax.axis_size("gy")
-    left = lax.ppermute(block[:, :, -1:], "gy", [(i, (i + 1) % count) for i in range(count)])
-    right = lax.ppermute(block[:, :, :1], "gy", [((i + 1) % count, i) for i in range(count)])
-    return jnp.concatenate([left, block, right], axis=2)
+def to_lines(block, odd):
+    planes, rows, cols, width = block.shape
+    zero = jnp.zeros_like(block[:, :, :1])
+    padded = jnp.concatenate([zero, block, zero], axis=2)
+    windows = jnp.stack([padded[:, :, b : b + cols] for b in range(3)], axis=3)
+    windows = jnp.where(odd, windows[:, :, ::-1], windows)
+    lines = lax.all_to_all(windows, "gx", split_axis=2, concat_axis=1, tiled=True)
+    return lines.reshape(rows * lax.axis_size("gx"), 3 * width)
 
 
-def to_lines(padded):
-    cols = padded.shape[2] - 2
-    windows = jnp.stack([padded[:, :, b : b + cols] for b in range(3)], axis=3)
-    return lax.all_to_all(windows, "gx", split_axis=2, concat_axis=1, tiled=True)
+def edge_lines(own):
+    n_gx, n_gy = lax.axis_size("gx"), lax.axis_size("gy")
+    last = n_gx - 1
+
+    def device(j, g):
+        return j * n_gy + g % n_gy
+
+    def edge(g, first):
+        return 0 if (g % 2 == 0) == first else last
+
+    rightward = [(device(edge(g, False), g), device(edge(g, False), g + 1)) for g in range(n_gy)]
+    leftward = [(device(edge(g, True), g), device(edge(g, True), g - 1)) for g in range(n_gy)]
+    from_left = lax.ppermute(own, ("gx", "gy"), rightward)
+    from_right = lax.ppermute(own, ("gx", "gy"), leftward)
+    return from_left, from_right
 
 
-def to_blocks(result, rows):
+def to_blocks(result, rows, odd):
     length, width = result.shape
     chunks = result.reshape(length // rows, rows, 1, width)
-    return lax.all_to_all(chunks, "gx", split_axis=0, concat_axis=2, tiled=True)
+    block = lax.all_to_all(chunks, "gx", split_axis=0, concat_axis=2, tiled=True)
+    return jnp.where(odd, block[:, :, ::-1], block)
 
 
 def line_kernel(x_ref, cw_ref, qw_ref, ow_ref, o_ref):
@@ -69,10 +84,13 @@
 
 
 def on_device(field, conv_weight, qkv_weight, out_weight):
-    lines = to_lines(padded_columns(field))
-    planes, length, _, taps, width = lines.shape
-    result = line_block(lines.reshape(length, taps * width), conv_weight, qkv_weight, out_weight)
-    return to_blocks(result, field.shape[1])
+    odd = lax.axis_index("gy") % 2 == 1
+    width = field.shape[3]
+    lines = to_lines(field, odd)
+    from_left, from_right = edge_lines(lines[:, width : 2 * width])
+    lines = lines + jnp.concatenate([from_left, jnp.zeros_like(from_left), from_right], axis=1)
+    result = line_block(lines, conv_weight, qkv_weight, out_weight)
+    return to_blocks(result, field.shape[1], odd)
 
 
 def solution(mesh):

time: 70.2 us -> 73.6 us (1.048)
  blocking collectives: 53.3 us -> 64.4 us
  starting transfers between devices: 8.95 us -> 1.34 us
  other arithmetic: 0.1 us -> 1.08 us
    all_to_all x1, blocking collectives: 20 us -> 30.8 us  [to_blocks(): lax.all_to_all(chunks, 'gx', split_axis=0, concat_axis=2, tiled=True)]
    ppermute x2, starting transfers between devices: 8.95 us -> 1.34 us  [the longest x1 0.67 us: edge_lines(): from_right = lax.ppermute(own, ('gx', 'gy'), leftward)]
    add x0 -> x1, other arithmetic: none -> 0.87 us  [on_device(): lines + jnp.concatenate([from_left, jnp.zeros_like(from_left), from_right...]
  transfers between devices with their start and end apart: 2 -> 2, of which waited for: 1 -> 0; matrix products, arithmetic and copies ran while one was open for 0% -> 0% of each run, Pallas kernels for 0% -> 0%
where the time goes in v7:
time: 73.6 us; the launch traced here: 73.4 us
  blocking collectives  64.4 us (88%)
  Pallas kernels  4.74 us (6%)
  local copies, waits for them, and re-layouts  1.71 us (2%)
  starting transfers between devices  1.34 us (2%)
  other arithmetic  1.08 us (1%)
    all_to_all x1, blocking collectives, to_lines(): lax.all_to_all(windows, 'gx', split_axis=2, concat_axis=1, tiled=True)  33.6 us
    all_to_all x1, blocking collectives, to_blocks(): lax.all_to_all(chunks, 'gx', split_axis=0, concat_axis=2, tiled=True)  30.8 us
    pallas_call x1, Pallas kernels, line_block(): pl.pallas_call(line_kernel, out_shape=jax.ShapeDtypeStruct((length, width...  4.74 us
  transfers between devices with their start and end apart: 2, of which 0 were waited for; matrix products, arithmetic and copies ran while one was open for 0% of the time, Pallas kernels for 0%

profile of v7, /device:TPU:1, one launch (start us, length us, event | category | flops | bytes accessed | tf_op | source)
XLA Modules:
  0.0 73.4 jit_solution(10016841119814130225)
XLA Ops:
  0.0 1.0 %copy.14 = bf16[1,8,64,128]{3,1,2,0:T(8,128)(2,1)S(1)} copy(bf16[1,8,64,128]{3,2,1,0:T(8,128)(2,1)} %param.4) | data formatting | bytes 262144 | tf_op args[0]
  1.0 0.1 pad_maximum_fusion
  1.1 0.1 reverse_select_fusion
  1.2 33.6 %all_to_all.33 = bf16[1,8,64,3,128]{4,1,3,0,2:T(8,128)(2,1)S(1)} all-to-all(bf16[1,8,64,3,128]{4,1,3,0,2:T(8,128)(2,1)S(1)} %reverse_select_fusion), channel_id=1, replica_groups=mesh['gx'=64,'gy'=8] {'gx'}, dimensions={2} | all-to-all | bytes 786432 | tf_op jit(solution)/shard_map/all_to_all | solution.py:18
  34.8 0.7 collective-permute-start.1
  35.5 0.7 collective-permute-start
  36.2 0.0 collective-permute-done.1
  36.2 0.0 collective-permute-done
  36.2 0.9 %maximum_add_fusion.x_ref = bf16[512,384]{1,0:T(8,128)(2,1)} fusion(bf16[512,128]{1,0:T(8,128)(2,1)S(1)} %collective-permute-done.1, bf16[512,128]{1,0:T(8,128)(2,1)S(1)} %collective-permute-done, bf16[384]{0:T(512)(128)(2,1)S(1)} %pad.3.clone, bf16[1,8,64,3,128]{4,1,3,0,2:T(8,128)(2,1)S(1)} %all_to_all.33), kind=kLoop, calls=%fused_computation.2 | loop fusion | flops 1572864 | bytes 1049344 | tf_op jit(solution)/shard_map/add | solution.py:91
  37.1 4.7 %shard_map.46 = bf16[512,128]{1,0:T(8,128)(2,1)} custom-call(bf16[512,384]{1,0:T(8,128)(2,1)} %maximum_add_fusion.x_ref, bf16[3,384,128]{2,1,0:T(8,128)(2,1)} %bitcast.26, bf16[128,384]{1,0:T(8,128)(2,1)} %qw_ref.1, bf16[128,128]{1,0:T(8,128)(2,1)} %ow_ref.1), custom_call_target="tpu_custom_call" | custom-call | tf_op jit(solution)/shard_map/pallas_call | solution.py:82
  41.9 30.8 %all_to_all.34 = bf16[64,8,1,128]{3,1,2,0:T(8,128)(2,1)S(1)} all-to-all(bf16[64,8,1,128]{3,1,2,0:T(8,128)(2,1)} %bitcast.25), channel_id=1, replica_groups=mesh['gx'=64,'gy'=8] {'gx'}, dimensions={0} | all-to-all | bytes 262144 | tf_op jit(solution)/shard_map/all_to_all | solution.py:42
  72.7 0.7 copy.11
  (5 shorter events, 0.1 us)
Async XLA Ops:
  34.8 1.4 %collective-permute-start.1 = (bf16[512,128]{1,0:T(8,128)(2,1)S(1)}, bf16[512,128]{1,0:T(8,128)(2,1)S(1)}, u32[]{:S(2)}, u32[]{:S(2)}) collective-permute-start(bf16[512,128]{1,0:T(8,128)(2,1)S(1)} %slice.14), channel_id=1, source_target_pairs={{0,7},{505,504},{2,1},{507,506},{4,3},{509,508},{6,5},{511,510}} | collective-permute-start | bytes 393224 | tf_op jit(solution)/shard_map/ppermute | solution.py:35
  35.5 0.7 collective-permute-start

commit v8 on v6

--- a/solution.py
+++ b/solution.py
@@ -12,9 +12,10 @@
 def padded_columns(block):
     count = lax.axis_size("gy")
     rims = lax.optimization_barrier(block)
-    left = lax.ppermute(rims[:, :, -1:], "gy", [(i, (i + 1) % count) for i in range(count)])
-    right = lax.ppermute(rims[:, :, :1], "gy", [((i + 1) % count, i) for i in range(count)])
-    return jnp.concatenate([left, block, right], axis=2)
+    tile = min(8, block.shape[2])
+    left = lax.ppermute(rims[:, :, -tile:], "gy", [(i, (i + 1) % count) for i in range(count)])
+    right = lax.ppermute(rims[:, :, :tile], "gy", [((i + 1) % count, i) for i in range(count)])
+    return jnp.concatenate([left[:, :, -1:], block, right[:, :, :1]], axis=2)
 
 
 def to_lines(padded):

time: 73.1 us -> 73.2 us (level)
  waiting for transfers between devices: 3.5 us -> 4.54 us
  local copies, waits for them, and re-layouts: 2.42 us -> 1.58 us
    ppermute x2, waiting for transfers between devices: 3.5 us -> 4.54 us  [the longest x1 4.54 us: padded_columns(): lax.ppermute(rims[:, :, -tile:], 'gy', [(i, (i + 1) % count) for i in ran...]
    unnamed x3 -> x5, local copies, waits for them, and re-layouts: 1 us -> 0.11 us
  transfers between devices with their start and end apart: 2 -> 2, of which waited for: 1 -> 1; matrix products, arithmetic and copies ran while one was open for 1% -> 0% of each run, Pallas kernels for 0% -> 0%
where the time goes in v8:
time: 73.2 us; the launch traced here: 73 us
  blocking collectives  53 us (72%)
  starting transfers between devices  8.95 us (12%)
  Pallas kernels  4.74 us (6%)
  waiting for transfers between devices  4.54 us (6%)
  local copies, waits for them, and re-layouts  1.58 us (2%)
    all_to_all x1, blocking collectives, to_lines(): lax.all_to_all(windows, 'gx', split_axis=2, concat_axis=1, tiled=True)  33.2 us
    all_to_all x1, blocking collectives, to_blocks(): return lax.all_to_all(chunks, 'gx', split_axis=0, concat_axis=2, tiled=True)  19.8 us
    ppermute x1, starting transfers between devices, padded_columns(): lax.ppermute(rims[:, :, :tile], 'gy', [((i + 1) % count, i) for i in rang...  7.02 us
    pallas_call x1, Pallas kernels, line_block(): pl.pallas_call(line_kernel, out_shape=jax.ShapeDtypeStruct((length, width...  4.74 us
    ppermute x1, waiting for transfers between devices, padded_columns(): lax.ppermute(rims[:, :, -tile:], 'gy', [(i, (i + 1) % count) for i in ran...  4.54 us
    ppermute x1, starting transfers between devices, padded_columns(): lax.ppermute(rims[:, :, -tile:], 'gy', [(i, (i + 1) % count) for i in ran...  1.92 us
  transfers between devices with their start and end apart: 2, of which 1 were waited for; matrix products, arithmetic and copies ran while one was open for 0% of the time, Pallas kernels for 0%

profile of v8, /device:TPU:1, one launch (start us, length us, event | category | flops | bytes accessed | tf_op | source)
XLA Modules:
  0.0 73.0 jit_solution(3988084106507402865)
XLA Ops:
  0.0 0.0 copy-start
  0.0 0.8 %fusion.2 = (bf16[1,8,8,128]{3,2,1,0:T(8,128)(2,1)S(1)}, bf16[1,8,8,128]{3,2,1,0:T(8,128)(2,1)S(1)}) fusion(bf16[1,8,64,128]{3,2,1,0:T(8,128)(2,1)} %param.4), kind=kLoop, calls=%fused_computation.6 | loop fusion | bytes 65536 | tf_op jit(solution)/shard_map/slice | solution.py:16
  0.8 7.0 %collective-permute-start.1 = (bf16[1,8,8,128]{3,1,2,0:T(8,128)(2,1)S(1)}, bf16[1,8,8,128]{3,1,2,0:T(8,128)(2,1)S(1)}, u32[]{:S(2)}, u32[]{:S(2)}) collective-permute-start(bf16[1,8,8,128]{3,1,2,0:T(8,128)(2,1)S(1)} %copy.15), channel_id=1, source_target_pairs={{1,0},{2,1},{3,2},{4,3},{5,4},{6,5},{7,6},{0,7},{9,8},{10,9},{11,1... | collective-permute-start | bytes 49160 | tf_op jit(solution)/shard_map/ppermute | solution.py:17
  7.8 1.9 %collective-permute-start = (bf16[1,8,8,128]{3,1,2,0:T(8,128)(2,1)S(1)}, bf16[1,8,8,128]{3,1,2,0:T(8,128)(2,1)S(1)}, u32[]{:S(2)}, u32[]{:S(2)}) collective-permute-start(bf16[1,8,8,128]{3,1,2,0:T(8,128)(2,1)S(1)} %copy.14), channel_id=1, source_target_pairs={{0,1},{1,2},{2,3},{3,4},{4,5},{5,6},{6,7},{7,0},{8,9},{9,10},{10,1... | collective-permute-start | bytes 49160 | tf_op jit(solution)/shard_map/ppermute | solution.py:16
  9.8 0.0 copy-done
  9.8 0.1 copy.18
  9.9 0.0 collective-permute-done.1
  9.9 4.5 %collective-permute-done = bf16[1,8,8,128]{3,1,2,0:T(8,128)(2,1)S(1)} collective-permute-done((bf16[1,8,8,128]{3,1,2,0:T(8,128)(2,1)S(1)}, bf16[1,8,8,128]{3,1,2,0:T(8,128)(2,1)S(1)}, u32[]{:S(2)}, u32[]{:S(2)}) %collective-permute-start) | collective-permute-done | bytes 16416 | tf_op jit(solution)/shard_map/ppermute | solution.py:16
  14.5 0.1 pad_maximum_fusion
  14.6 33.2 %all_to_all.33 = bf16[1,8,64,3,128]{4,1,3,0,2:T(8,128)(2,1)} all-to-all(bf16[1,8,64,3,128]{4,1,3,0,2:T(8,128)(2,1)S(1)} %pad_maximum_fusion), channel_id=1, replica_groups=mesh['gx'=64,'gy'=8] {'gx'}, dimensions={2} | all-to-all | bytes 786432 | tf_op jit(solution)/shard_map/all_to_all | solution.py:24
  47.8 4.7 %shard_map.46 = bf16[512,128]{1,0:T(8,128)(2,1)} custom-call(bf16[512,384]{1,0:T(8,128)(2,1)} %bitcast.21, bf16[3,384,128]{2,1,0:T(8,128)(2,1)} %bitcast.25, bf16[128,384]{1,0:T(8,128)(2,1)} %qw_ref.1, bf16[128,128]{1,0:T(8,128)(2,1)} %ow_ref.1), custom_call_target="tpu_custom_call" | custom-call | tf_op jit(solution)/shard_map/pallas_call | solution.py:69
  52.5 19.8 %all_to_all.34 = bf16[64,8,1,128]{3,1,2,0:T(8,128)(2,1)S(1)} all-to-all(bf16[64,8,1,128]{3,1,2,0:T(8,128)(2,1)} %bitcast.24), channel_id=1, replica_groups=mesh['gx'=64,'gy'=8] {'gx'}, dimensions={0} | all-to-all | bytes 262144 | tf_op jit(solution)/shard_map/all_to_all | solution.py:30
  72.3 0.7 copy.13
  (5 shorter events, 0.0 us)
Async XLA Ops:
  0.0 9.8 %copy-start = (bf16[1,8,64,128]{3,2,1,0:T(8,128)(2,1)S(1)}, bf16[1,8,64,128]{3,2,1,0:T(8,128)(2,1)}, u32[]{:S(2)}) copy-start(bf16[1,8,64,128]{3,2,1,0:T(8,128)(2,1)} %param.4) | copy-start | bytes 393220
  0.8 9.1 %collective-permute-start.1 = (bf16[1,8,8,128]{3,1,2,0:T(8,128)(2,1)S(1)}, bf16[1,8,8,128]{3,1,2,0:T(8,128)(2,1)S(1)}, u32[]{:S(2)}, u32[]{:S(2)}) collective-permute-start(bf16[1,8,8,128]{3,1,2,0:T(8,128)(2,1)S(1)} %copy.15), channel_id=1, source_target_pairs={{1,0},{2,1},{3,2},{4,3},{5,4},{6,5},{7,6},{0,7},{9,8},{10,9},{11,1... | collective-permute-start | bytes 49160 | tf_op jit(solution)/shard_map/ppermute | solution.py:17
  7.8 6.6 %collective-permute-start = (bf16[1,8,8,128]{3,1,2,0:T(8,128)(2,1)S(1)}, bf16[1,8,8,128]{3,1,2,0:T(8,128)(2,1)S(1)}, u32[]{:S(2)}, u32[]{:S(2)}) collective-permute-start(bf16[1,8,8,128]{3,1,2,0:T(8,128)(2,1)S(1)} %copy.14), channel_id=1, source_target_pairs={{0,1},{1,2},{2,3},{3,4},{4,5},{5,6},{6,7},{7,0},{8,9},{9,10},{10,1... | collective-permute-start | bytes 49160 | tf_op jit(solution)/shard_map/ppermute | solution.py:16

commit v9 on v5

--- a/solution.py
+++ b/solution.py
@@ -11,8 +11,13 @@
 
 def padded_columns(block):
     count = lax.axis_size("gy")
-    left = lax.ppermute(block[:, :, -1:], "gy", [(i, (i + 1) % count) for i in range(count)])
-    right = lax.ppermute(block[:, :, :1], "gy", [((i + 1) % count, i) for i in range(count)])
+    me = lax.axis_index("gy")
+    peer = lax.broadcasted_iota(jnp.int32, (count, 1, 1, 1), 0)
+    last, first = block[0, :, -1:], block[0, :, :1]
+    chunks = jnp.where(peer == (me + 1) % count, last, jnp.where(peer == (me + count - 1) % count, first, 0))
+    got = lax.all_to_all(chunks.astype(block.dtype), "gy", split_axis=0, concat_axis=0, tiled=True)
+    left = lax.dynamic_index_in_dim(got, (me + count - 1) % count, 0, keepdims=True)
+    right = lax.dynamic_index_in_dim(got, (me + 1) % count, 0, keepdims=True)
     return jnp.concatenate([left, block, right], axis=2)
 
 

time: 70.2 us -> 72.3 us (1.030)
  waiting for transfers between devices: 0.71 us -> 5.07 us
  starting transfers between devices: 8.95 us -> 6.66 us
    ppermute x2 -> x0, starting transfers between devices: 8.95 us -> none  [the longest x1 5 us: padded_columns(): lax.ppermute(block[:, :, :1], 'gy', [((i + 1) % count, i) for i in range(...]
    all_to_all x0 -> x1, starting transfers between devices: none -> 6.66 us  [padded_columns(): lax.all_to_all(chunks.astype(block.dtype), 'gy', split_axis=0, concat_axi...]
    all_to_all x0 -> x1, waiting for transfers between devices: none -> 5.07 us  [padded_columns(): lax.all_to_all(chunks.astype(block.dtype), 'gy', split_axis=0, concat_axi...]
  transfers between devices with their start and end apart: 2 -> 1, of which waited for: 1 -> 1; matrix products, arithmetic and copies ran while one was open for 0% -> 0% of each run, Pallas kernels for 0% -> 0%
where the time goes in v9:
time: 72.3 us; the launch traced here: 72 us
  blocking collectives  53 us (73%)
  starting transfers between devices  6.66 us (9%)
  waiting for transfers between devices  5.07 us (7%)
  Pallas kernels  4.74 us (7%)
  local copies, waits for them, and re-layouts  1.68 us (2%)
  other arithmetic  0.8 us (1%)
    all_to_all x1, blocking collectives, to_lines(): lax.all_to_all(windows, 'gx', split_axis=2, concat_axis=1, tiled=True)  33.2 us
    all_to_all x1, blocking collectives, to_blocks(): return lax.all_to_all(chunks, 'gx', split_axis=0, concat_axis=2, tiled=True)  19.8 us
    all_to_all x1, starting transfers between devices, padded_columns(): lax.all_to_all(chunks.astype(block.dtype), 'gy', split_axis=0, concat_axi...  6.66 us
    all_to_all x1, waiting for transfers between devices, padded_columns(): lax.all_to_all(chunks.astype(block.dtype), 'gy', split_axis=0, concat_axi...  5.07 us
    pallas_call x1, Pallas kernels, line_block(): pl.pallas_call(line_kernel, out_shape=jax.ShapeDtypeStruct((length, width...  4.74 us
  transfers between devices with their start and end apart: 1, of which 1 were waited for; matrix products, arithmetic and copies ran while one was open for 0% of the time, Pallas kernels for 0%

profile of v9, /device:TPU:1, one launch (start us, length us, event | category | flops | bytes accessed | tf_op | source)
XLA Modules:
  0.0 72.0 jit_solution(16909751955521464167)
XLA Ops:
  0.0 1.0 %copy.20 = bf16[1,8,64,128]{3,1,2,0:T(8,128)(2,1)S(1)} copy(bf16[1,8,64,128]{3,2,1,0:T(8,128)(2,1)} %param.4) | data formatting | bytes 262144 | tf_op args[0]
  1.0 0.7 select_select_fusion
  1.7 6.7 %all-to-all-start = ((bf16[8,8,1,128]{3,1,2,0:T(8,128)(2,1)}), bf16[8,8,1,128]{3,1,2,0:T(8,128)(2,1)S(1)}, u32[]{:S(2)}, u32[]{:S(2)}) async-start(bf16[8,8,1,128]{3,1,2,0:T(8,128)(2,1)} %select_select_fusion), calls=%async_computation | async-start | bytes 32768 | tf_op jit(solution)/shard_map/all_to_all | solution.py:18
  8.4 5.1 %all-to-all-done = bf16[8,8,1,128]{3,1,2,0:T(8,128)(2,1)S(1)} async-done(((bf16[8,8,1,128]{3,1,2,0:T(8,128)(2,1)}), bf16[8,8,1,128]{3,1,2,0:T(8,128)(2,1)S(1)}, u32[]{:S(2)}, u32[]{:S(2)}) %all-to-all-start) | async-done | bytes 16416 | tf_op jit(solution)/shard_map/all_to_all | solution.py:18
  13.5 0.1 pad_maximum_fusion
  13.6 33.2 %all_to_all.38 = bf16[1,8,64,3,128]{4,1,3,0,2:T(8,128)(2,1)} all-to-all(bf16[1,8,64,3,128]{4,1,3,0,2:T(8,128)(2,1)S(1)} %pad_maximum_fusion), channel_id=1, replica_groups=mesh['gx'=64,'gy'=8] {'gx'}, dimensions={2} | all-to-all | bytes 786432 | tf_op jit(solution)/shard_map/all_to_all | solution.py:27
  46.8 4.7 %shard_map.46 = bf16[512,128]{1,0:T(8,128)(2,1)} custom-call(bf16[512,384]{1,0:T(8,128)(2,1)} %bitcast.25, bf16[3,384,128]{2,1,0:T(8,128)(2,1)} %bitcast.29, bf16[128,384]{1,0:T(8,128)(2,1)} %qw_ref.1, bf16[128,128]{1,0:T(8,128)(2,1)} %ow_ref.1), custom_call_target="tpu_custom_call" | custom-call | tf_op jit(solution)/shard_map/pallas_call | solution.py:72
  51.5 19.8 %all_to_all.39 = bf16[64,8,1,128]{3,1,2,0:T(8,128)(2,1)S(1)} all-to-all(bf16[64,8,1,128]{3,1,2,0:T(8,128)(2,1)} %bitcast.28), channel_id=1, replica_groups=mesh['gx'=64,'gy'=8] {'gx'}, dimensions={0} | all-to-all | bytes 262144 | tf_op jit(solution)/shard_map/all_to_all | solution.py:33
  71.3 0.7 copy.17
  (4 shorter events, 0.0 us)
Async XLA Ops:
  1.7 11.7 %all-to-all-start = ((bf16[8,8,1,128]{3,1,2,0:T(8,128)(2,1)}), bf16[8,8,1,128]{3,1,2,0:T(8,128)(2,1)S(1)}, u32[]{:S(2)}, u32[]{:S(2)}) async-start(bf16[8,8,1,128]{3,1,2,0:T(8,128)(2,1)} %select_select_fusion), calls=%async_computation | async-start | bytes 32768 | tf_op jit(solution)/shard_map/all_to_all | solution.py:18

commit v10 on v5

--- a/solution.py
+++ b/solution.py
@@ -7,6 +7,7 @@
 
 HEADS = 4
 HEAD = 32
+BLOCKS = 2
 
 
 def padded_columns(block):
@@ -46,16 +47,22 @@
     zero = jnp.zeros_like(keyed)
     keys = jnp.concatenate([jnp.where(head_of == h, keyed, zero) for h in range(HEADS)], axis=0)
     values = jnp.concatenate([jnp.where(head_of == h, valued, zero) for h in range(HEADS)], axis=0)
-    scores = lax.dot_general(query, keys, (((1,), (1,)), ((), ())), preferred_element_type=jnp.float32)
     scale = 1.0 / jnp.sqrt(jnp.float32(HEAD))
-    weights, inverse = [], jnp.zeros((length, width), jnp.float32)
-    for h in range(HEADS):
-        s = scores[:, h * length:(h + 1) * length] * scale
-        e = jnp.exp(s - jnp.max(s, axis=1, keepdims=True))
-        weights.append(e.astype(jnp.bfloat16))
-        inverse = jnp.where(head_of == h, 1.0 / jnp.sum(e, axis=1, keepdims=True), inverse)
-    mixed = jnp.dot(jnp.concatenate(weights, axis=1), values, preferred_element_type=jnp.float32)
-    attended = (mixed * inverse).astype(jnp.bfloat16)
+    rows = length // BLOCKS
+    parts = []
+    for r in range(BLOCKS):
+        part = slice(r * rows, (r + 1) * rows)
+        scores = lax.dot_general(query[part], keys, (((1,), (1,)), ((), ())),
+                                 preferred_element_type=jnp.float32)
+        weights, inverse = [], jnp.zeros((rows, width), jnp.float32)
+        for h in range(HEADS):
+            s = scores[:, h * length:(h + 1) * length] * scale
+            e = jnp.exp(s - jnp.max(s, axis=1, keepdims=True))
+            weights.append(e.astype(jnp.bfloat16))
+            inverse = jnp.where(head_of[part] == h, 1.0 / jnp.sum(e, axis=1, keepdims=True), inverse)
+        mixed = jnp.dot(jnp.concatenate(weights, axis=1), values, preferred_element_type=jnp.float32)
+        parts.append((mixed * inverse).astype(jnp.bfloat16))
+    attended = jnp.concatenate(parts, axis=0)
     total = stem + jnp.dot(attended, ow_ref[...], preferred_element_type=jnp.float32)
     o_ref[...] = total.astype(o_ref.dtype)
 

time: 70.2 us -> 70 us (level)
  no operation moved by 1% of the time
where the time goes in v10:
time: 70 us; the launch traced here: 69.4 us
  blocking collectives  53.3 us (76%)
  starting transfers between devices  8.95 us (13%)
  Pallas kernels  4.59 us (7%)
  local copies, waits for them, and re-layouts  1.67 us (2%)
  waiting for transfers between devices  0.71 us (1%)
    all_to_all x1, blocking collectives, to_lines(): lax.all_to_all(windows, 'gx', split_axis=2, concat_axis=1, tiled=True)  33.3 us
    all_to_all x1, blocking collectives, to_blocks(): return lax.all_to_all(chunks, 'gx', split_axis=0, concat_axis=2, tiled=True)  20 us
    ppermute x1, starting transfers between devices, padded_columns(): lax.ppermute(block[:, :, :1], 'gy', [((i + 1) % count, i) for i in range(...  5 us
    pallas_call x1, Pallas kernels, line_block(): pl.pallas_call(line_kernel, out_shape=jax.ShapeDtypeStruct((length, width...  4.59 us
    ppermute x1, starting transfers between devices, padded_columns(): lax.ppermute(block[:, :, -1:], 'gy', [(i, (i + 1) % count) for i in range...  3.95 us
  transfers between devices with their start and end apart: 2, of which 1 were waited for; matrix products, arithmetic and copies ran while one was open for 0% of the time, Pallas kernels for 0%

profile of v10, /device:TPU:1, one launch (start us, length us, event | category | flops | bytes accessed | tf_op | source)
XLA Modules:
  0.0 69.4 jit_solution(11363521668983035025)
XLA Ops:
  0.0 1.0 %copy.16 = bf16[1,8,64,128]{3,1,2,0:T(8,128)(2,1)S(1)} copy(bf16[1,8,64,128]{3,2,1,0:T(8,128)(2,1)} %param.4) | data formatting | bytes 262144 | tf_op args[0]
  1.0 3.9 %collective-permute-start = (bf16[1,8,1,128]{3,1,2,0:T(8,128)(2,1)S(1)}, bf16[1,8,1,128]{3,1,2,0:T(8,128)(2,1)S(1)}, u32[]{:S(2)}, u32[]{:S(2)}) collective-permute-start(bf16[1,8,1,128]{3,1,2,0:T(8,128)(2,1)S(1)} %get-tuple-element.7), channel_id=1, source_target_pairs={{0,1},{1,2},{2,3},{3,4},{4,5},{5,6},{6,7},{7,0},{8,9},{9,10},{10,1... | collective-permute-start | bytes 6152 | tf_op jit(solution)/shard_map/ppermute | solution.py:15
  5.0 5.0 %collective-permute-start.1 = (bf16[1,8,1,128]{3,1,2,0:T(8,128)(2,1)S(1)}, bf16[1,8,1,128]{3,1,2,0:T(8,128)(2,1)S(1)}, u32[]{:S(2)}, u32[]{:S(2)}) collective-permute-start(bf16[1,8,1,128]{3,1,2,0:T(8,128)(2,1)S(1)} %get-tuple-element.8), channel_id=1, source_target_pairs={{1,0},{2,1},{3,2},{4,3},{5,4},{6,5},{7,6},{0,7},{9,8},{10,9},{11,1... | collective-permute-start | bytes 6152 | tf_op jit(solution)/shard_map/ppermute | solution.py:16
  10.0 0.0 collective-permute-done
  10.0 0.7 %collective-permute-done.1 = bf16[1,8,1,128]{3,1,2,0:T(8,128)(2,1)S(1)} collective-permute-done((bf16[1,8,1,128]{3,1,2,0:T(8,128)(2,1)S(1)}, bf16[1,8,1,128]{3,1,2,0:T(8,128)(2,1)S(1)}, u32[]{:S(2)}, u32[]{:S(2)}) %collective-permute-start.1) | collective-permute-done | bytes 2080 | tf_op jit(solution)/shard_map/ppermute | solution.py:16
  10.7 0.1 pad_maximum_fusion
  10.8 33.3 %all_to_all.33 = bf16[1,8,64,3,128]{4,1,3,0,2:T(8,128)(2,1)} all-to-all(bf16[1,8,64,3,128]{4,1,3,0,2:T(8,128)(2,1)S(1)} %pad_maximum_fusion), channel_id=1, replica_groups=mesh['gx'=64,'gy'=8] {'gx'}, dimensions={2} | all-to-all | bytes 786432 | tf_op jit(solution)/shard_map/all_to_all | solution.py:23
  44.1 4.6 %shard_map.46 = bf16[512,128]{1,0:T(8,128)(2,1)} custom-call(bf16[512,384]{1,0:T(8,128)(2,1)} %bitcast.21, bf16[3,384,128]{2,1,0:T(8,128)(2,1)} %bitcast.25, bf16[128,384]{1,0:T(8,128)(2,1)} %qw_ref.1, bf16[128,128]{1,0:T(8,128)(2,1)} %ow_ref.1), custom_call_target="tpu_custom_call" | custom-call | tf_op jit(solution)/shard_map/pallas_call | solution.py:74
  48.7 20.0 %all_to_all.34 = bf16[64,8,1,128]{3,1,2,0:T(8,128)(2,1)S(1)} all-to-all(bf16[64,8,1,128]{3,1,2,0:T(8,128)(2,1)} %bitcast.24), channel_id=1, replica_groups=mesh['gx'=64,'gy'=8] {'gx'}, dimensions={0} | all-to-all | bytes 262144 | tf_op jit(solution)/shard_map/all_to_all | solution.py:29
  68.7 0.7 copy.13
  (2 shorter events, 0.0 us)
Async XLA Ops:
  1.0 9.0 %collective-permute-start = (bf16[1,8,1,128]{3,1,2,0:T(8,128)(2,1)S(1)}, bf16[1,8,1,128]{3,1,2,0:T(8,128)(2,1)S(1)}, u32[]{:S(2)}, u32[]{:S(2)}) collective-permute-start(bf16[1,8,1,128]{3,1,2,0:T(8,128)(2,1)S(1)} %get-tuple-element.7), channel_id=1, source_target_pairs={{0,1},{1,2},{2,3},{3,4},{4,5},{5,6},{6,7},{7,0},{8,9},{9,10},{10,1... | collective-permute-start | bytes 6152 | tf_op jit(solution)/shard_map/ppermute | solution.py:15
  5.0 5.7 %collective-permute-start.1 = (bf16[1,8,1,128]{3,1,2,0:T(8,128)(2,1)S(1)}, bf16[1,8,1,128]{3,1,2,0:T(8,128)(2,1)S(1)}, u32[]{:S(2)}, u32[]{:S(2)}) collective-permute-start(bf16[1,8,1,128]{3,1,2,0:T(8,128)(2,1)S(1)} %get-tuple-element.8), channel_id=1, source_target_pairs={{1,0},{2,1},{3,2},{4,3},{5,4},{6,5},{7,6},{0,7},{9,8},{10,9},{11,1... | collective-permute-start | bytes 6152 | tf_op jit(solution)/shard_map/ppermute | solution.py:16

commit v11 on v10

--- a/solution.py
+++ b/solution.py
@@ -32,27 +32,30 @@
 def line_kernel(x_ref, cw_ref, qw_ref, ow_ref, o_ref):
     length = x_ref.shape[0]
     width = o_ref.shape[1]
+    rows = length // BLOCKS
     x = x_ref[...]
     taps = jnp.dot(x, jnp.concatenate([cw_ref[a] for a in range(3)], axis=1),
                    preferred_element_type=jnp.float32)
     stem = (taps[:, width:2 * width] + pltpu.roll(taps[:, :width], 1, 0)
             + pltpu.roll(taps[:, 2 * width:], length - 1, 0))
-    mean = jnp.mean(stem, axis=-1, keepdims=True)
-    centred = stem - mean
-    varia = jnp.mean(centred * centred, axis=-1, keepdims=True)
-    normed = (centred / jnp.sqrt(varia + 1e-05)).astype(jnp.bfloat16)
-    qkv = jnp.dot(normed, qw_ref[...], preferred_element_type=jnp.float32).astype(jnp.bfloat16)
-    query, keyed, valued = qkv[:, :width], qkv[:, width:2 * width], qkv[:, 2 * width:]
+    halves = [slice(r * rows, (r + 1) * rows) for r in range(BLOCKS)]
+    qkvs = []
+    for part in halves:
+        piece = stem[part]
+        mean = jnp.mean(piece, axis=-1, keepdims=True)
+        centred = piece - mean
+        varia = jnp.mean(centred * centred, axis=-1, keepdims=True)
+        normed = (centred / jnp.sqrt(varia + 1e-05)).astype(jnp.bfloat16)
+        qkvs.append(jnp.dot(normed, qw_ref[...], preferred_element_type=jnp.float32).astype(jnp.bfloat16))
+    qkv = jnp.concatenate(qkvs, axis=0)
+    keyed, valued = qkv[:, width:2 * width], qkv[:, 2 * width:]
     head_of = lax.broadcasted_iota(jnp.int32, (length, width), 1) // HEAD
     zero = jnp.zeros_like(keyed)
     keys = jnp.concatenate([jnp.where(head_of == h, keyed, zero) for h in range(HEADS)], axis=0)
     values = jnp.concatenate([jnp.where(head_of == h, valued, zero) for h in range(HEADS)], axis=0)
     scale = 1.0 / jnp.sqrt(jnp.float32(HEAD))
-    rows = length // BLOCKS
-    parts = []
-    for r in range(BLOCKS):
-        part = slice(r * rows, (r + 1) * rows)
-        scores = lax.dot_general(query[part], keys, (((1,), (1,)), ((), ())),
+    for r, part in enumerate(halves):
+        scores = lax.dot_general(qkvs[r][:, :width], keys, (((1,), (1,)), ((), ())),
                                  preferred_element_type=jnp.float32)
         weights, inverse = [], jnp.zeros((rows, width), jnp.float32)
         for h in range(HEADS):
@@ -61,10 +64,9 @@
             weights.append(e.astype(jnp.bfloat16))
             inverse = jnp.where(head_of[part] == h, 1.0 / jnp.sum(e, axis=1, keepdims=True), inverse)
         mixed = jnp.dot(jnp.concatenate(weights, axis=1), values, preferred_element_type=jnp.float32)
-        parts.append((mixed * inverse).astype(jnp.bfloat16))
-    attended = jnp.concatenate(parts, axis=0)
-    total = stem + jnp.dot(attended, ow_ref[...], preferred_element_type=jnp.float32)
-    o_ref[...] = total.astype(o_ref.dtype)
+        attended = (mixed * inverse).astype(jnp.bfloat16)
+        total = stem[part] + jnp.dot(attended, ow_ref[...], preferred_element_type=jnp.float32)
+        o_ref[part, :] = total.astype(o_ref.dtype)
 
 
 def line_block(lines, conv_weight, qkv_weight, out_weight):

time: 70 us -> 70.2 us (level)
  no operation moved by 1% of the time
where the time goes in v11:
time: 70.2 us; the launch traced here: 69.5 us
  blocking collectives  53.3 us (76%)
  starting transfers between devices  8.95 us (13%)
  Pallas kernels  4.75 us (7%)
  local copies, waits for them, and re-layouts  1.67 us (2%)
  waiting for transfers between devices  0.71 us (1%)
    all_to_all x1, blocking collectives, to_lines(): lax.all_to_all(windows, 'gx', split_axis=2, concat_axis=1, tiled=True)  33.3 us
    all_to_all x1, blocking collectives, to_blocks(): return lax.all_to_all(chunks, 'gx', split_axis=0, concat_axis=2, tiled=True)  20 us
    ppermute x1, starting transfers between devices, padded_columns(): lax.ppermute(block[:, :, :1], 'gy', [((i + 1) % count, i) for i in range(...  5 us
    pallas_call x1, Pallas kernels, line_block(): pl.pallas_call(line_kernel, out_shape=jax.ShapeDtypeStruct((length, width...  4.75 us
    ppermute x1, starting transfers between devices, padded_columns(): lax.ppermute(block[:, :, -1:], 'gy', [(i, (i + 1) % count) for i in range...  3.95 us
  transfers between devices with their start and end apart: 2, of which 1 were waited for; matrix products, arithmetic and copies ran while one was open for 0% of the time, Pallas kernels for 0%

profile of v11, /device:TPU:1, one launch (start us, length us, event | category | flops | bytes accessed | tf_op | source)
XLA Modules:
  0.0 69.5 jit_solution(652713246352341439)
XLA Ops:
  0.0 1.0 %copy.16 = bf16[1,8,64,128]{3,1,2,0:T(8,128)(2,1)S(1)} copy(bf16[1,8,64,128]{3,2,1,0:T(8,128)(2,1)} %param.4) | data formatting | bytes 262144 | tf_op args[0]
  1.0 3.9 %collective-permute-start = (bf16[1,8,1,128]{3,1,2,0:T(8,128)(2,1)S(1)}, bf16[1,8,1,128]{3,1,2,0:T(8,128)(2,1)S(1)}, u32[]{:S(2)}, u32[]{:S(2)}) collective-permute-start(bf16[1,8,1,128]{3,1,2,0:T(8,128)(2,1)S(1)} %get-tuple-element.7), channel_id=1, source_target_pairs={{0,1},{1,2},{2,3},{3,4},{4,5},{5,6},{6,7},{7,0},{8,9},{9,10},{10,1... | collective-permute-start | bytes 6152 | tf_op jit(solution)/shard_map/ppermute | solution.py:15
  5.0 5.0 %collective-permute-start.1 = (bf16[1,8,1,128]{3,1,2,0:T(8,128)(2,1)S(1)}, bf16[1,8,1,128]{3,1,2,0:T(8,128)(2,1)S(1)}, u32[]{:S(2)}, u32[]{:S(2)}) collective-permute-start(bf16[1,8,1,128]{3,1,2,0:T(8,128)(2,1)S(1)} %get-tuple-element.8), channel_id=1, source_target_pairs={{1,0},{2,1},{3,2},{4,3},{5,4},{6,5},{7,6},{0,7},{9,8},{10,9},{11,1... | collective-permute-start | bytes 6152 | tf_op jit(solution)/shard_map/ppermute | solution.py:16
  10.0 0.0 collective-permute-done
  10.0 0.7 %collective-permute-done.1 = bf16[1,8,1,128]{3,1,2,0:T(8,128)(2,1)S(1)} collective-permute-done((bf16[1,8,1,128]{3,1,2,0:T(8,128)(2,1)S(1)}, bf16[1,8,1,128]{3,1,2,0:T(8,128)(2,1)S(1)}, u32[]{:S(2)}, u32[]{:S(2)}) %collective-permute-start.1) | collective-permute-done | bytes 2080 | tf_op jit(solution)/shard_map/ppermute | solution.py:16
  10.7 0.1 pad_maximum_fusion
  10.8 33.3 %all_to_all.33 = bf16[1,8,64,3,128]{4,1,3,0,2:T(8,128)(2,1)} all-to-all(bf16[1,8,64,3,128]{4,1,3,0,2:T(8,128)(2,1)S(1)} %pad_maximum_fusion), channel_id=1, replica_groups=mesh['gx'=64,'gy'=8] {'gx'}, dimensions={2} | all-to-all | bytes 786432 | tf_op jit(solution)/shard_map/all_to_all | solution.py:23
  44.1 4.8 %shard_map.46 = bf16[512,128]{1,0:T(8,128)(2,1)} custom-call(bf16[512,384]{1,0:T(8,128)(2,1)} %bitcast.21, bf16[3,384,128]{2,1,0:T(8,128)(2,1)} %bitcast.25, bf16[128,384]{1,0:T(8,128)(2,1)} %qw_ref.1, bf16[128,128]{1,0:T(8,128)(2,1)} %ow_ref.1), custom_call_target="tpu_custom_call" | custom-call | tf_op jit(solution)/shard_map/pallas_call | solution.py:76
  48.8 20.0 %all_to_all.34 = bf16[64,8,1,128]{3,1,2,0:T(8,128)(2,1)S(1)} all-to-all(bf16[64,8,1,128]{3,1,2,0:T(8,128)(2,1)} %bitcast.24), channel_id=1, replica_groups=mesh['gx'=64,'gy'=8] {'gx'}, dimensions={0} | all-to-all | bytes 262144 | tf_op jit(solution)/shard_map/all_to_all | solution.py:29
  68.8 0.7 copy.13
  (2 shorter events, 0.0 us)
Async XLA Ops:
  1.0 9.0 %collective-permute-start = (bf16[1,8,1,128]{3,1,2,0:T(8,128)(2,1)S(1)}, bf16[1,8,1,128]{3,1,2,0:T(8,128)(2,1)S(1)}, u32[]{:S(2)}, u32[]{:S(2)}) collective-permute-start(bf16[1,8,1,128]{3,1,2,0:T(8,128)(2,1)S(1)} %get-tuple-element.7), channel_id=1, source_target_pairs={{0,1},{1,2},{2,3},{3,4},{4,5},{5,6},{6,7},{7,0},{8,9},{9,10},{10,1... | collective-permute-start | bytes 6152 | tf_op jit(solution)/shard_map/ppermute | solution.py:15
  5.0 5.7 %collective-permute-start.1 = (bf16[1,8,1,128]{3,1,2,0:T(8,128)(2,1)S(1)}, bf16[1,8,1,128]{3,1,2,0:T(8,128)(2,1)S(1)}, u32[]{:S(2)}, u32[]{:S(2)}) collective-permute-start(bf16[1,8,1,128]{3,1,2,0:T(8,128)(2,1)S(1)} %get-tuple-element.8), channel_id=1, source_target_pairs={{1,0},{2,1},{3,2},{4,3},{5,4},{6,5},{7,6},{0,7},{9,8},{10,9},{11,1... | collective-permute-start | bytes 6152 | tf_op jit(solution)/shard_map/ppermute | solution.py:16

commit v12 on v10

--- a/solution.py
+++ b/solution.py
@@ -49,7 +49,6 @@
     values = jnp.concatenate([jnp.where(head_of == h, valued, zero) for h in range(HEADS)], axis=0)
     scale = 1.0 / jnp.sqrt(jnp.float32(HEAD))
     rows = length // BLOCKS
-    parts = []
     for r in range(BLOCKS):
         part = slice(r * rows, (r + 1) * rows)
         scores = lax.dot_general(query[part], keys, (((1,), (1,)), ((), ())),
@@ -61,10 +60,9 @@
             weights.append(e.astype(jnp.bfloat16))
             inverse = jnp.where(head_of[part] == h, 1.0 / jnp.sum(e, axis=1, keepdims=True), inverse)
         mixed = jnp.dot(jnp.concatenate(weights, axis=1), values, preferred_element_type=jnp.float32)
-        parts.append((mixed * inverse).astype(jnp.bfloat16))
-    attended = jnp.concatenate(parts, axis=0)
-    total = stem + jnp.dot(attended, ow_ref[...], preferred_element_type=jnp.float32)
-    o_ref[...] = total.astype(o_ref.dtype)
+        attended = (mixed * inverse).astype(jnp.bfloat16)
+        total = stem[part] + jnp.dot(attended, ow_ref[...], preferred_element_type=jnp.float32)
+        o_ref[part, :] = total.astype(o_ref.dtype)
 
 
 def line_block(lines, conv_weight, qkv_weight, out_weight):

time: 70 us -> 70.2 us (level)
  no operation moved by 1% of the time
where the time goes in v12:
time: 70.2 us; the launch traced here: 69.5 us
  blocking collectives  53.3 us (76%)
  starting transfers between devices  8.95 us (13%)
  Pallas kernels  4.75 us (7%)
  local copies, waits for them, and re-layouts  1.67 us (2%)
  waiting for transfers between devices  0.71 us (1%)
    all_to_all x1, blocking collectives, to_lines(): lax.all_to_all(windows, 'gx', split_axis=2, concat_axis=1, tiled=True)  33.3 us
    all_to_all x1, blocking collectives, to_blocks(): return lax.all_to_all(chunks, 'gx', split_axis=0, concat_axis=2, tiled=True)  20 us
    ppermute x1, starting transfers between devices, padded_columns(): lax.ppermute(block[:, :, :1], 'gy', [((i + 1) % count, i) for i in range(...  5 us
    pallas_call x1, Pallas kernels, line_block(): pl.pallas_call(line_kernel, out_shape=jax.ShapeDtypeStruct((length, width...  4.75 us
    ppermute x1, starting transfers between devices, padded_columns(): lax.ppermute(block[:, :, -1:], 'gy', [(i, (i + 1) % count) for i in range...  3.95 us
  transfers between devices with their start and end apart: 2, of which 1 were waited for; matrix products, arithmetic and copies ran while one was open for 0% of the time, Pallas kernels for 0%

profile of v12, /device:TPU:1, one launch (start us, length us, event | category | flops | bytes accessed | tf_op | source)
XLA Modules:
  0.0 69.5 jit_solution(3182741267234251711)
XLA Ops:
  0.0 1.0 %copy.16 = bf16[1,8,64,128]{3,1,2,0:T(8,128)(2,1)S(1)} copy(bf16[1,8,64,128]{3,2,1,0:T(8,128)(2,1)} %param.4) | data formatting | bytes 262144 | tf_op args[0]
  1.0 3.9 %collective-permute-start = (bf16[1,8,1,128]{3,1,2,0:T(8,128)(2,1)S(1)}, bf16[1,8,1,128]{3,1,2,0:T(8,128)(2,1)S(1)}, u32[]{:S(2)}, u32[]{:S(2)}) collective-permute-start(bf16[1,8,1,128]{3,1,2,0:T(8,128)(2,1)S(1)} %get-tuple-element.7), channel_id=1, source_target_pairs={{0,1},{1,2},{2,3},{3,4},{4,5},{5,6},{6,7},{7,0},{8,9},{9,10},{10,1... | collective-permute-start | bytes 6152 | tf_op jit(solution)/shard_map/ppermute | solution.py:15
  5.0 5.0 %collective-permute-start.1 = (bf16[1,8,1,128]{3,1,2,0:T(8,128)(2,1)S(1)}, bf16[1,8,1,128]{3,1,2,0:T(8,128)(2,1)S(1)}, u32[]{:S(2)}, u32[]{:S(2)}) collective-permute-start(bf16[1,8,1,128]{3,1,2,0:T(8,128)(2,1)S(1)} %get-tuple-element.8), channel_id=1, source_target_pairs={{1,0},{2,1},{3,2},{4,3},{5,4},{6,5},{7,6},{0,7},{9,8},{10,9},{11,1... | collective-permute-start | bytes 6152 | tf_op jit(solution)/shard_map/ppermute | solution.py:16
  10.0 0.0 collective-permute-done
  10.0 0.7 %collective-permute-done.1 = bf16[1,8,1,128]{3,1,2,0:T(8,128)(2,1)S(1)} collective-permute-done((bf16[1,8,1,128]{3,1,2,0:T(8,128)(2,1)S(1)}, bf16[1,8,1,128]{3,1,2,0:T(8,128)(2,1)S(1)}, u32[]{:S(2)}, u32[]{:S(2)}) %collective-permute-start.1) | collective-permute-done | bytes 2080 | tf_op jit(solution)/shard_map/ppermute | solution.py:16
  10.7 0.1 pad_maximum_fusion
  10.8 33.3 %all_to_all.33 = bf16[1,8,64,3,128]{4,1,3,0,2:T(8,128)(2,1)} all-to-all(bf16[1,8,64,3,128]{4,1,3,0,2:T(8,128)(2,1)S(1)} %pad_maximum_fusion), channel_id=1, replica_groups=mesh['gx'=64,'gy'=8] {'gx'}, dimensions={2} | all-to-all | bytes 786432 | tf_op jit(solution)/shard_map/all_to_all | solution.py:23
  44.1 4.7 %shard_map.46 = bf16[512,128]{1,0:T(8,128)(2,1)} custom-call(bf16[512,384]{1,0:T(8,128)(2,1)} %bitcast.21, bf16[3,384,128]{2,1,0:T(8,128)(2,1)} %bitcast.25, bf16[128,384]{1,0:T(8,128)(2,1)} %qw_ref.1, bf16[128,128]{1,0:T(8,128)(2,1)} %ow_ref.1), custom_call_target="tpu_custom_call" | custom-call | tf_op jit(solution)/shard_map/pallas_call | solution.py:72
  48.8 20.0 %all_to_all.34 = bf16[64,8,1,128]{3,1,2,0:T(8,128)(2,1)S(1)} all-to-all(bf16[64,8,1,128]{3,1,2,0:T(8,128)(2,1)} %bitcast.24), channel_id=1, replica_groups=mesh['gx'=64,'gy'=8] {'gx'}, dimensions={0} | all-to-all | bytes 262144 | tf_op jit(solution)/shard_map/all_to_all | solution.py:29
  68.8 0.7 copy.13
  (2 shorter events, 0.0 us)
Async XLA Ops:
  1.0 9.0 %collective-permute-start = (bf16[1,8,1,128]{3,1,2,0:T(8,128)(2,1)S(1)}, bf16[1,8,1,128]{3,1,2,0:T(8,128)(2,1)S(1)}, u32[]{:S(2)}, u32[]{:S(2)}) collective-permute-start(bf16[1,8,1,128]{3,1,2,0:T(8,128)(2,1)S(1)} %get-tuple-element.7), channel_id=1, source_target_pairs={{0,1},{1,2},{2,3},{3,4},{4,5},{5,6},{6,7},{7,0},{8,9},{9,10},{10,1... | collective-permute-start | bytes 6152 | tf_op jit(solution)/shard_map/ppermute | solution.py:15
  5.0 5.7 %collective-permute-start.1 = (bf16[1,8,1,128]{3,1,2,0:T(8,128)(2,1)S(1)}, bf16[1,8,1,128]{3,1,2,0:T(8,128)(2,1)S(1)}, u32[]{:S(2)}, u32[]{:S(2)}) collective-permute-start(bf16[1,8,1,128]{3,1,2,0:T(8,128)(2,1)S(1)} %get-tuple-element.8), channel_id=1, source_target_pairs={{1,0},{2,1},{3,2},{4,3},{5,4},{6,5},{7,6},{0,7},{9,8},{10,9},{11,1... | collective-permute-start | bytes 6152 | tf_op jit(solution)/shard_map/ppermute | solution.py:16

commit v13 on v10

--- a/solution.py
+++ b/solution.py
@@ -10,17 +10,30 @@
 BLOCKS = 2
 
 
+def swap_kernel(x_ref, o_ref):
+    o_ref[...] = jnp.swapaxes(x_ref[...].astype(jnp.float32), 0, 1).astype(o_ref.dtype)
+
+
+def column_major(block):
+    rows, cols, width = block.shape
+    vm = pl.BlockSpec(memory_space=pltpu.VMEM)
+    return pl.pallas_call(swap_kernel, out_shape=jax.ShapeDtypeStruct((cols, rows, width), block.dtype),
+        in_specs=[vm], out_specs=vm)(block)
+
+
 def padded_columns(block):
     count = lax.axis_size("gy")
-    left = lax.ppermute(block[:, :, -1:], "gy", [(i, (i + 1) % count) for i in range(count)])
-    right = lax.ppermute(block[:, :, :1], "gy", [((i + 1) % count, i) for i in range(count)])
-    return jnp.concatenate([left, block, right], axis=2)
+    columns = column_major(block[0])
+    left = lax.ppermute(columns[-1:], "gy", [(i, (i + 1) % count) for i in range(count)])
+    right = lax.ppermute(columns[:1], "gy", [((i + 1) % count, i) for i in range(count)])
+    return jnp.concatenate([left, columns, right], axis=0)
 
 
 def to_lines(padded):
-    cols = padded.shape[2] - 2
-    windows = jnp.stack([padded[:, :, b : b + cols] for b in range(3)], axis=3)
-    return lax.all_to_all(windows, "gx", split_axis=2, concat_axis=1, tiled=True)
+    cols, rows, width = padded.shape[0] - 2, padded.shape[1], padded.shape[2]
+    windows = jnp.stack([padded[b : b + cols] for b in range(3)], axis=2)
+    lines = lax.all_to_all(windows, "gx", split_axis=0, concat_axis=0, tiled=True)
+    return lines.reshape(cols * rows, 3 * width)
 
 
 def to_blocks(result, rows):
@@ -77,8 +90,7 @@
 
 def on_device(field, conv_weight, qkv_weight, out_weight):
     lines = to_lines(padded_columns(field))
-    planes, length, _, taps, width = lines.shape
-    result = line_block(lines.reshape(length, taps * width), conv_weight, qkv_weight, out_weight)
+    result = line_block(lines, conv_weight, qkv_weight, out_weight)
     return to_blocks(result, field.shape[1])
 
 

time: 70 us -> 72.5 us (1.036)
  Pallas kernels: 4.59 us -> 6.2 us
  other arithmetic: 0.1 us -> 1.05 us
    pallas_call x0 -> x1, Pallas kernels: none -> 1.62 us  [column_major(): pl.pallas_call(swap_kernel, out_shape=jax.ShapeDtypeStruct((cols, rows, w...]
    unnamed x1 -> x2, local copies, waits for them, and re-layouts: 0.99 us -> 0.01 us
    another operation x2, other arithmetic: 0.1 us -> 1.05 us  [to_lines(): windows = jnp.stack([padded[b:b + cols] for b in range(3)], axis=2)]
where the time goes in v13:
time: 72.5 us; the launch traced here: 71.8 us
  blocking collectives  53.3 us (74%)
  starting transfers between devices  9.06 us (12%)
  Pallas kernels  6.2 us (9%)
  local copies, waits for them, and re-layouts  1.45 us (2%)
  other arithmetic  1.05 us (1%)
    all_to_all x1, blocking collectives, to_lines(): lax.all_to_all(windows, 'gx', split_axis=0, concat_axis=0, tiled=True)  33.3 us
    all_to_all x1, blocking collectives, to_blocks(): return lax.all_to_all(chunks, 'gx', split_axis=0, concat_axis=2, tiled=True)  20 us
    ppermute x1, starting transfers between devices, padded_columns(): lax.ppermute(columns[:1], 'gy', [((i + 1) % count, i) for i in range(coun...  5.13 us
    pallas_call x1, Pallas kernels, line_block(): pl.pallas_call(line_kernel, out_shape=jax.ShapeDtypeStruct((length, width...  4.58 us
    ppermute x1, starting transfers between devices, padded_columns(): lax.ppermute(columns[-1:], 'gy', [(i, (i + 1) % count) for i in range(cou...  3.94 us
    pallas_call x1, Pallas kernels, column_major(): pl.pallas_call(swap_kernel, out_shape=jax.ShapeDtypeStruct((cols, rows, w...  1.62 us
  transfers between devices with their start and end apart: 2, of which 1 were waited for; matrix products, arithmetic and copies ran while one was open for 0% of the time, Pallas kernels for 0%

profile of v13, /device:TPU:1, one launch (start us, length us, event | category | flops | bytes accessed | tf_op | source)
XLA Modules:
  0.0 71.8 jit_solution(14682346318108151120)
XLA Ops:
  0.0 1.6 %shard_map.46 = bf16[64,8,128]{2,1,0:T(8,128)(2,1)} custom-call(bf16[8,64,128]{2,1,0:T(8,128)(2,1)} %bitcast.21), custom_call_target="tpu_custom_call" | custom-call | tf_op jit(solution)/shard_map/pallas_call | solution.py:20
  1.6 0.7 fusion.2
  2.3 3.9 %collective-permute-start = (bf16[1,8,128]{2,1,0:T(8,128)(2,1)S(1)}, bf16[1,8,128]{2,1,0:T(8,128)(2,1)S(1)}, u32[]{:S(2)}, u32[]{:S(2)}) collective-permute-start(bf16[1,8,128]{2,1,0:T(8,128)(2,1)S(1)} %get-tuple-element.7), channel_id=1, source_target_pairs={{0,1},{1,2},{2,3},{3,4},{4,5},{5,6},{6,7},{7,0},{8,9},{9,10},{10,1... | collective-permute-start | bytes 6152 | tf_op jit(solution)/shard_map/ppermute | solution.py:27
  6.3 0.0 copy-start
  6.3 5.1 %collective-permute-start.1 = (bf16[1,8,128]{2,1,0:T(8,128)(2,1)S(1)}, bf16[1,8,128]{2,1,0:T(8,128)(2,1)S(1)}, u32[]{:S(2)}, u32[]{:S(2)}) collective-permute-start(bf16[1,8,128]{2,1,0:T(8,128)(2,1)S(1)} %get-tuple-element.8), channel_id=1, source_target_pairs={{1,0},{2,1},{3,2},{4,3},{5,4},{6,5},{7,6},{0,7},{9,8},{10,9},{11,1... | collective-permute-start | bytes 6152 | tf_op jit(solution)/shard_map/ppermute | solution.py:28
  11.4 0.0 collective-permute-done
  11.4 0.7 collective-permute-done.1
  12.1 1.0 %fusion.1 = (bf16[64,8,1,128]{3,1,0,2:T(8,128)(2,1)S(1)}, bf16[64,8,1,128]{3,1,0,2:T(8,128)(2,1)S(1)}) fusion(bf16[64,8,128]{2,1,0:T(8,128)(2,1)} %shard_map.46, bf16[1,8,128]{2,1,0:T(8,128)(2,1)S(1)} %collective-permute-done, bf16[1,8,128]{2,1,0:T(8,128)(2,1)S(1)} %collective-permute-done.1), kind=kLoop, calls=%fused_computation.4 | loop fusion | flops 131072 | bytes 397312 | tf_op jit(solution)/shard_map/stack | solution.py:34
  13.1 0.0 copy-done
  13.2 0.1 copy.7
  13.3 33.3 %all_to_all.23 = bf16[64,8,3,128]{3,1,2,0:T(8,128)(2,1)} all-to-all(bf16[64,8,3,128]{3,1,2,0:T(8,128)(2,1)S(1)} %copy.7), channel_id=1, replica_groups=mesh['gx'=64,'gy'=8] {'gx'}, dimensions={0} | all-to-all | bytes 786432 | tf_op jit(solution)/shard_map/all_to_all | solution.py:35
  46.6 4.6 %shard_map.47 = bf16[512,128]{1,0:T(8,128)(2,1)} custom-call(bf16[512,384]{1,0:T(8,128)(2,1)} %bitcast.16, bf16[3,384,128]{2,1,0:T(8,128)(2,1)} %bitcast.20, bf16[128,384]{1,0:T(8,128)(2,1)} %qw_ref.1, bf16[128,128]{1,0:T(8,128)(2,1)} %ow_ref.1), custom_call_target="tpu_custom_call" | custom-call | tf_op jit(solution)/shard_map/pallas_call | solution.py:87
  51.2 20.0 %all_to_all.24 = bf16[64,8,1,128]{3,1,2,0:T(8,128)(2,1)S(1)} all-to-all(bf16[64,8,1,128]{3,1,2,0:T(8,128)(2,1)} %bitcast.19), channel_id=1, replica_groups=mesh['gx'=64,'gy'=8] {'gx'}, dimensions={0} | all-to-all | bytes 262144 | tf_op jit(solution)/shard_map/all_to_all | solution.py:42
  71.2 0.7 copy.9
  (1 shorter events, 0.0 us)
Async XLA Ops:
  2.3 9.1 %collective-permute-start = (bf16[1,8,128]{2,1,0:T(8,128)(2,1)S(1)}, bf16[1,8,128]{2,1,0:T(8,128)(2,1)S(1)}, u32[]{:S(2)}, u32[]{:S(2)}) collective-permute-start(bf16[1,8,128]{2,1,0:T(8,128)(2,1)S(1)} %get-tuple-element.7), channel_id=1, source_target_pairs={{0,1},{1,2},{2,3},{3,4},{4,5},{5,6},{6,7},{7,0},{8,9},{9,10},{10,1... | collective-permute-start | bytes 6152 | tf_op jit(solution)/shard_map/ppermute | solution.py:27
  6.3 6.9 %copy-start = (bf16[64,8,128]{2,1,0:T(8,128)(2,1)S(1)}, bf16[64,8,128]{2,1,0:T(8,128)(2,1)}, u32[]{:S(2)}) copy-start(bf16[64,8,128]{2,1,0:T(8,128)(2,1)} %shard_map.46) | copy-start | bytes 393220
  6.3 5.8 %collective-permute-start.1 = (bf16[1,8,128]{2,1,0:T(8,128)(2,1)S(1)}, bf16[1,8,128]{2,1,0:T(8,128)(2,1)S(1)}, u32[]{:S(2)}, u32[]{:S(2)}) collective-permute-start(bf16[1,8,128]{2,1,0:T(8,128)(2,1)S(1)} %get-tuple-element.8), channel_id=1, source_target_pairs={{1,0},{2,1},{3,2},{4,3},{5,4},{6,5},{7,6},{0,7},{9,8},{10,9},{11,1... | collective-permute-start | bytes 6152 | tf_op jit(solution)/shard_map/ppermute | solution.py:28

commit v14 on v10

--- a/solution.py
+++ b/solution.py
@@ -69,10 +69,11 @@
 
 def line_block(lines, conv_weight, qkv_weight, out_weight):
     length = lines.shape[0]; width = out_weight.shape[1]
-    cw = conv_weight.reshape(3, 3 * width, width)
+    cw, qw, ow = (pltpu.with_memory_space_constraint(w, pltpu.VMEM)
+                  for w in (conv_weight.reshape(3, 3 * width, width), qkv_weight, out_weight))
     vm = pl.BlockSpec(memory_space=pltpu.VMEM)
     return pl.pallas_call(line_kernel, out_shape=jax.ShapeDtypeStruct((length, width), jnp.bfloat16),
-        in_specs=[vm]*4, out_specs=vm)(lines, cw, qkv_weight, out_weight)
+        in_specs=[vm]*4, out_specs=vm)(lines, cw, qw, ow)
 
 
 def on_device(field, conv_weight, qkv_weight, out_weight):

time: 70 us -> 70.1 us (level)
  no operation moved by 1% of the time
where the time goes in v14:
time: 70.1 us; the launch traced here: 69.4 us
  blocking collectives  53.4 us (76%)
  starting transfers between devices  8.95 us (13%)
  Pallas kernels  4.47 us (6%)
  local copies, waits for them, and re-layouts  1.69 us (2%)
  waiting for transfers between devices  0.71 us (1%)
    all_to_all x1, blocking collectives, to_lines(): lax.all_to_all(windows, 'gx', split_axis=2, concat_axis=1, tiled=True)  33.4 us
    all_to_all x1, blocking collectives, to_blocks(): return lax.all_to_all(chunks, 'gx', split_axis=0, concat_axis=2, tiled=True)  20 us
    ppermute x1, starting transfers between devices, padded_columns(): lax.ppermute(block[:, :, :1], 'gy', [((i + 1) % count, i) for i in range(...  5 us
    pallas_call x1, Pallas kernels, line_block(): pl.pallas_call(line_kernel, out_shape=jax.ShapeDtypeStruct((length, width...  4.47 us
    ppermute x1, starting transfers between devices, padded_columns(): lax.ppermute(block[:, :, -1:], 'gy', [(i, (i + 1) % count) for i in range...  3.95 us
  transfers between devices with their start and end apart: 2, of which 1 were waited for; matrix products, arithmetic and copies ran while one was open for 0% of the time, Pallas kernels for 0%

profile of v14, /device:TPU:1, one launch (start us, length us, event | category | flops | bytes accessed | tf_op | source)
XLA Modules:
  0.0 69.4 jit_solution(872074708474708659)
XLA Ops:
  0.0 1.0 %copy.16 = bf16[1,8,64,128]{3,1,2,0:T(8,128)(2,1)S(1)} copy(bf16[1,8,64,128]{3,2,1,0:T(8,128)(2,1)} %param.4) | data formatting | bytes 262144 | tf_op args[0]
  1.0 3.9 %collective-permute-start = (bf16[1,8,1,128]{3,1,2,0:T(8,128)(2,1)S(1)}, bf16[1,8,1,128]{3,1,2,0:T(8,128)(2,1)S(1)}, u32[]{:S(2)}, u32[]{:S(2)}) collective-permute-start(bf16[1,8,1,128]{3,1,2,0:T(8,128)(2,1)S(1)} %get-tuple-element.7), channel_id=1, source_target_pairs={{0,1},{1,2},{2,3},{3,4},{4,5},{5,6},{6,7},{7,0},{8,9},{9,10},{10,1... | collective-permute-start | bytes 6152 | tf_op jit(solution)/shard_map/ppermute | solution.py:15
  5.0 5.0 %collective-permute-start.1 = (bf16[1,8,1,128]{3,1,2,0:T(8,128)(2,1)S(1)}, bf16[1,8,1,128]{3,1,2,0:T(8,128)(2,1)S(1)}, u32[]{:S(2)}, u32[]{:S(2)}) collective-permute-start(bf16[1,8,1,128]{3,1,2,0:T(8,128)(2,1)S(1)} %get-tuple-element.8), channel_id=1, source_target_pairs={{1,0},{2,1},{3,2},{4,3},{5,4},{6,5},{7,6},{0,7},{9,8},{10,9},{11,1... | collective-permute-start | bytes 6152 | tf_op jit(solution)/shard_map/ppermute | solution.py:16
  10.0 0.0 collective-permute-done
  10.0 0.7 %collective-permute-done.1 = bf16[1,8,1,128]{3,1,2,0:T(8,128)(2,1)S(1)} collective-permute-done((bf16[1,8,1,128]{3,1,2,0:T(8,128)(2,1)S(1)}, bf16[1,8,1,128]{3,1,2,0:T(8,128)(2,1)S(1)}, u32[]{:S(2)}, u32[]{:S(2)}) %collective-permute-start.1) | collective-permute-done | bytes 2080 | tf_op jit(solution)/shard_map/ppermute | solution.py:16
  10.7 0.1 pad_maximum_fusion
  10.8 0.0 copy-start
  10.8 0.0 copy-start.1
  10.8 0.0 copy-start.2
  10.8 33.4 %all_to_all.33 = bf16[1,8,64,3,128]{4,1,3,0,2:T(8,128)(2,1)} all-to-all(bf16[1,8,64,3,128]{4,1,3,0,2:T(8,128)(2,1)S(1)} %pad_maximum_fusion), channel_id=1, replica_groups=mesh['gx'=64,'gy'=8] {'gx'}, dimensions={2} | all-to-all | bytes 786432 | tf_op jit(solution)/shard_map/all_to_all | solution.py:23
  44.3 0.0 copy-done
  44.3 0.0 copy-done.1
  44.3 0.0 copy-done.2
  44.3 4.5 %shard_map.46 = bf16[512,128]{1,0:T(8,128)(2,1)} custom-call(bf16[512,384]{1,0:T(8,128)(2,1)} %bitcast.22, bf16[3,384,128]{2,1,0:T(8,128)(2,1)S(1)} %bitcast.21, bf16[128,384]{1,0:T(8,128)(2,1)S(1)} %copy-done.1, bf16[128,128]{1,0:T(8,128)(2,1)S(1)} %copy-done.2), custom_call_target="tpu_custom_call" | custom-call | tf_op jit(solution)/shard_map/pallas_call | solution.py:75
  48.7 20.0 %all_to_all.34 = bf16[64,8,1,128]{3,1,2,0:T(8,128)(2,1)S(1)} all-to-all(bf16[64,8,1,128]{3,1,2,0:T(8,128)(2,1)} %bitcast.25), channel_id=1, replica_groups=mesh['gx'=64,'gy'=8] {'gx'}, dimensions={0} | all-to-all | bytes 262144 | tf_op jit(solution)/shard_map/all_to_all | solution.py:29
  68.7 0.7 copy.13
  (2 shorter events, 0.0 us)
Async XLA Ops:
  1.0 9.0 %collective-permute-start = (bf16[1,8,1,128]{3,1,2,0:T(8,128)(2,1)S(1)}, bf16[1,8,1,128]{3,1,2,0:T(8,128)(2,1)S(1)}, u32[]{:S(2)}, u32[]{:S(2)}) collective-permute-start(bf16[1,8,1,128]{3,1,2,0:T(8,128)(2,1)S(1)} %get-tuple-element.7), channel_id=1, source_target_pairs={{0,1},{1,2},{2,3},{3,4},{4,5},{5,6},{6,7},{7,0},{8,9},{9,10},{10,1... | collective-permute-start | bytes 6152 | tf_op jit(solution)/shard_map/ppermute | solution.py:15
  5.0 5.7 %collective-permute-start.1 = (bf16[1,8,1,128]{3,1,2,0:T(8,128)(2,1)S(1)}, bf16[1,8,1,128]{3,1,2,0:T(8,128)(2,1)S(1)}, u32[]{:S(2)}, u32[]{:S(2)}) collective-permute-start(bf16[1,8,1,128]{3,1,2,0:T(8,128)(2,1)S(1)} %get-tuple-element.8), channel_id=1, source_target_pairs={{1,0},{2,1},{3,2},{4,3},{5,4},{6,5},{7,6},{0,7},{9,8},{10,9},{11,1... | collective-permute-start | bytes 6152 | tf_op jit(solution)/shard_map/ppermute | solution.py:16
  10.8 33.5 %copy-start = (bf16[3,3,128,128]{3,2,1,0:T(8,128)(2,1)S(1)}, bf16[3,3,128,128]{3,2,1,0:T(8,128)(2,1)}, u32[]{:S(2)}) copy-start(bf16[3,3,128,128]{3,2,1,0:T(8,128)(2,1)} %param.5) | copy-start | bytes 884740
  10.8 33.5 %copy-start.1 = (bf16[128,384]{1,0:T(8,128)(2,1)S(1)}, bf16[128,384]{1,0:T(8,128)(2,1)}, u32[]{:S(2)}) copy-start(bf16[128,384]{1,0:T(8,128)(2,1)} %qw_ref.1) | copy-start | bytes 294916
  10.8 33.4 %copy-start.2 = (bf16[128,128]{1,0:T(8,128)(2,1)S(1)}, bf16[128,128]{1,0:T(8,128)(2,1)}, u32[]{:S(2)}) copy-start(bf16[128,128]{1,0:T(8,128)(2,1)} %ow_ref.1) | copy-start | bytes 98308
